TPU v7x, 8 devices: a whole 2x2x1 slice. The times are simulated.
8 devices in a mesh: dp: 2 (over z, y), ctx: 4 (over x, core).
Axes of the slice: x: 2, y: 2, z: 1, core: 2. Of those that a mesh axis runs over, the one named last changes fastest.
Arguments:
- queries: bfloat16 [64, 512, 12, 128], P('dp', 'ctx'), parts along dimension 0
- keys: bfloat16 [64, 512, 1, 128], P('dp', 'ctx'), parts along dimension 0
- values: bfloat16 [64, 512, 1, 128], P('dp', 'ctx'), parts along dimension 0
- grad_out: bfloat16 [64, 512, 12, 128], P('dp', 'ctx'), parts along dimension 0
Outputs:
- output 1: bfloat16 [64, 512, 12, 128], P('dp', 'ctx'), parts along dimension 0
- output 2: bfloat16 [64, 512, 12, 128], P('dp', 'ctx'), parts along dimension 0
- output 3: bfloat16 [64, 512, 1, 128], P('dp', 'ctx'), parts along dimension 0
- output 4: bfloat16 [64, 512, 1, 128], P('dp', 'ctx'), parts along dimension 0
There are 2 independent parts. A program takes and returns all parts, laid end to end along the dimension named above; each array names one.
All inputs are finite; a program needn't handle non-finite values.
Results may differ from a plain program's by a relative error of at most 0.0071199.
Values are sent between devices in bfloat16 or wider.
A program may use at most 1 GiB of HBM per device.

v0:
```python
import jax
import jax.numpy as jnp
from jax import lax
from jax.sharding import PartitionSpec as P

NEG_BIG = -1e30


def block_scores(q_heads, k_blk, q_start, k_start, scale):
    scores = jnp.einsum("bihgd,bjhd->bhgij", q_heads, k_blk, preferred_element_type=jnp.float32) * scale
    q_pos = q_start + jnp.arange(q_heads.shape[1])
    k_pos = k_start + jnp.arange(k_blk.shape[1])
    return jnp.where(q_pos[:, None] >= k_pos[None, :], scores, NEG_BIG)


def attend_forward(q_heads, k_all, v_all, dev_idx, scale):
    n_batch, c_len, n_kv, n_grp, d_head = q_heads.shape
    stat_shape = (n_batch, n_kv, n_grp, c_len)
    q_start = dev_idx * c_len

    def loop_body(key_idx, carry):
        m_run, l_run, acc_run = carry
        k_blk = lax.dynamic_index_in_dim(k_all, key_idx, 1, keepdims=False)
        v_blk = lax.dynamic_index_in_dim(v_all, key_idx, 1, keepdims=False)
        scores = block_scores(q_heads, k_blk, q_start, key_idx * c_len, scale)
        m_new = jnp.maximum(m_run, scores.max(axis=-1))
        rescale = jnp.exp(m_run - m_new)
        weights = jnp.exp(scores - m_new[..., None])
        l_new = l_run * rescale + weights.sum(axis=-1)
        acc_new = acc_run * rescale[..., None] + jnp.einsum("bhgij,bjhd->bhgid", weights.astype(jnp.bfloat16), v_blk, preferred_element_type=jnp.float32)
        return m_new, l_new, acc_new

    init_carry = (jnp.full(stat_shape, NEG_BIG, jnp.float32), jnp.zeros(stat_shape, jnp.float32), jnp.zeros(stat_shape + (d_head,), jnp.float32))
    m_fin, l_fin, acc_fin = lax.fori_loop(0, dev_idx + 1, loop_body, init_carry)
    out_heads = jnp.transpose((acc_fin / l_fin[..., None]).astype(jnp.bfloat16), (0, 3, 1, 2, 4))
    return out_heads, m_fin + jnp.log(l_fin)


def attend_backward(q_heads, do_heads, out_heads, lse_row, k_all, v_all, dev_idx, scale):
    c_len = q_heads.shape[1]
    q_start = dev_idx * c_len
    delta_row = jnp.einsum("bihgd,bihgd->bhgi", do_heads, out_heads, preferred_element_type=jnp.float32)

    def loop_body(key_idx, carry):
        dq_acc, dk_all, dv_all = carry
        k_blk = lax.dynamic_index_in_dim(k_all, key_idx, 1, keepdims=False)
        v_blk = lax.dynamic_index_in_dim(v_all, key_idx, 1, keepdims=False)
        scores = block_scores(q_heads, k_blk, q_start, key_idx * c_len, scale)
        weights = jnp.exp(scores - lse_row[..., None])
        dv_blk = jnp.einsum("bhgij,bihgd->bjhd", weights.astype(jnp.bfloat16), do_heads, preferred_element_type=jnp.float32)
        dp_blk = jnp.einsum("bihgd,bjhd->bhgij", do_heads, v_blk, preferred_element_type=jnp.float32)
        ds_half = (weights * (dp_blk - delta_row[..., None])).astype(jnp.bfloat16)
        dq_acc = dq_acc + jnp.einsum("bhgij,bjhd->bihgd", ds_half, k_blk, preferred_element_type=jnp.float32)
        dk_blk = jnp.einsum("bhgij,bihgd->bjhd", ds_half, q_heads, preferred_element_type=jnp.float32)
        dk_all = lax.dynamic_update_index_in_dim(dk_all, dk_blk, key_idx, 1)
        dv_all = lax.dynamic_update_index_in_dim(dv_all, dv_blk, key_idx, 1)
        return dq_acc, dk_all, dv_all

    acc_zero = jnp.zeros(k_all.shape, jnp.float32)
    init_carry = (jnp.zeros(q_heads.shape, jnp.float32), acc_zero, acc_zero)
    return lax.fori_loop(0, dev_idx + 1, loop_body, init_carry)


def solution(mesh):
    part_spec = P("dp", "ctx")

    def local_step(queries, keys, values, grad_out):
        n_batch, c_len, n_q, d_head = queries.shape
        n_kv = keys.shape[2]
        scale = d_head ** -0.5
        dev_idx = lax.axis_index("ctx")
        head_shape = (n_batch, c_len, n_kv, n_q // n_kv, d_head)
        q_heads = queries.reshape(head_shape)
        do_heads = grad_out.reshape(head_shape)
        k_all = lax.all_gather(keys, "ctx", axis=1)
        v_all = lax.all_gather(values, "ctx", axis=1)
        out_heads, lse_row = attend_forward(q_heads, k_all, v_all, dev_idx, scale)
        dq_acc, dk_all, dv_all = attend_backward(q_heads, do_heads, out_heads, lse_row, k_all, v_all, dev_idx, scale)
        dk_sum = lax.psum_scatter(dk_all, "ctx", scatter_dimension=1)
        dv_sum = lax.psum_scatter(dv_all, "ctx", scatter_dimension=1)
        attn_out = out_heads.reshape(n_batch, c_len, n_q, d_head)
        grad_q = (dq_acc * scale).astype(jnp.bfloat16).reshape(n_batch, c_len, n_q, d_head)
        grad_k = (dk_sum * scale).astype(jnp.bfloat16)
        grad_v = dv_sum.astype(jnp.bfloat16)
        return attn_out, grad_q, grad_k, grad_v

    return jax.shard_map(local_step, mesh=mesh, in_specs=(part_spec,) * 4, out_specs=(part_spec,) * 4, check_vma=False)
```

profile of v0, /device:TPU:0, one launch (start us, length us, event | category | flops | bytes accessed | tf_op | source)
XLA Modules:
  0.0 825.3 jit_solution(13738495985862090165)
XLA Ops:
  7.2 0.7 all-gather.5.cloned.1.call-update
  7.9 0.7 all-gather.7.cloned.1.call-update
  8.7 35.2 %all-gather.5.cloned.1.call-done = bf16[32,512,1,128]{3,1,0,2:T(8,128)(2,1)} async-done(((bf16[32,128,1,128]{3,1,0,2:T(8,128)(2,1)}), bf16[32,512,1,128]{3,1,0,2:T(8,128)(2,1)}) %all-gather.5.cloned.1.call-update) | async-done | bytes 4194320 | tf_op jit(solution)/shard_map/all_gather | solution.py:75
  43.9 4.8 copy.27
  48.7 28.3 %all-gather.7.cloned.1.call-done = bf16[32,512,1,128]{3,1,0,2:T(8,128)(2,1)} async-done(((bf16[32,128,1,128]{3,1,0,2:T(8,128)(2,1)}), bf16[32,512,1,128]{3,1,0,2:T(8,128)(2,1)}) %all-gather.7.cloned.1.call-update) | async-done | bytes 4194320 | tf_op jit(solution)/shard_map/all_gather | solution.py:76
  76.9 4.7 copy.28
  81.7 11.5 %broadcast_in_dim.47 = f32[32,1,12,128,128]{4,3,2,0,1:T(8,128)} broadcast(f32[]{:T(128)} %constant.55.clone.1), dimensions={} | broadcast | bytes 25165828 | tf_op jit(solution)/shard_map/broadcast_in_dim | solution.py:33
  93.2 52.7 %while.28 = (s32[]{:T(128)}, f32[32,1,12,128]{3,2,0,1:T(8,128)S(1)}, f32[32,1,12,128]{3,2,0,1:T(8,128)S(1)}, f32[32,1,12,128,128]{4,3,2,0,1:T(8,128)}, s32[]{:T(...) while((s32[]{:T(128)}, ...), condition=%wide.region_3.4_spmd, body=%wide.region_0.3_spmd.sunk | while | flops 3303178496 | bytes 143722704 | solution.py:34
  93.2 0.1 broadcast_compare_fusion.4
  93.3 13.5 %fusion.89 = (f32[32,12,128]{2,1,0:T(8,128)S(1)}, f32[32,128,128,12]{2,1,3,0:T(8,128)}) fusion(pred[128,128]{0,1:T(8,128)(4,1)S(1)} %broadcast_compare_fusion.4, bf16[32,128,1,12,128]{4,1,3,0,2:T(8,128)(2,1)} %get-tuple-element.400, bf16[32,4,128,1,128]{4,2,0,3,1:T(8,128)(2,1)} %get-tuple-element.399, s32[]{:T(128)S(6)} %select_n.57), kind=kOutput, calls=%fused_computation.5.clone.1 | convolution fusion | flops 1629437952 | bytes 39010308 | tf_op jit(solution)/shard_map/while/body/bihgd,bjhd->bhgij/dot_general | solution.py:10
  106.9 11.4 %fusion.91 = f32[32,12,128]{2,1,0:T(8,128)S(1)} fusion(f32[32,128,128,12]{2,1,3,0:T(8,128)} %get-tuple-element.351, f32[32,12,128]{2,1,0:T(8,128)S(1)} %bitcast.243, pred[128,128]{0,1:T(8,128)(4,1)S(1)} %broadcast_compare_fusion.4), kind=kLoop, calls=%fused_computation.4.clone.1 | loop fusion | flops 25116672 | bytes 25575424 | tf_op jit(solution)/shard_map/while/body/reduce_sum | solution.py:29
  118.3 0.2 bitcast_add_fusion.6
  118.5 27.4 %bitcast_add_fusion.7 = f32[32,1,12,128,128]{4,3,2,0,1:T(8,128)} fusion(f32[32,1,12,128,128]{4,3,2,0,1:T(8,128)} %get-tuple-element.383, f32[32,12,128]{2,1,0:T(8,128)S(1)} %get-tuple-element.352, f32[32,128,128,12]{2,1,3,0:T(8,128)} %get-tuple-element.351, f32[32,12,128]{2,1,0:T(8,128)S(1)} %bitcast.244, ...), kind=kOutput, calls=%fused_computation.1.clone.1 | convolution fusion | flops 1648361472 | bytes 76955648 | tf_op jit(solution)/shard_map/while/body/bhgij,bjhd->bhgid/dot_general | solution.py:30
  146.0 20.4 %fusion.64 = f32[32,12,128]{2,1,0:T(8,128)S(1)} fusion(bf16[32,128,12,128]{3,1,2,0:T(8,128)(2,1)} %param.11, f32[32,1,12,128,128]{4,3,2,0,1:T(8,128)} %get-tuple-element.119, f32[32,12,128]{2,1,0:T(8,128)S(1)} %bitcast.245), kind=kLoop, calls=%fused_computation.68 | loop fusion | flops 37699584 | bytes 38141952 | tf_op jit(solution)/shard_map/bihgd,bihgd->bhgi/dot_general | solution.py:42
  166.4 11.5 %broadcast_in_dim.48 = f32[32,128,1,12,128]{1,4,3,0,2:T(8,128)} broadcast(f32[]{:T(128)} %constant.55.clone.1), dimensions={} | broadcast | bytes 25165828 | tf_op jit(solution)/shard_map/broadcast_in_dim | solution.py:60
  178.0 4.3 broadcast_in_dim.49
  182.3 4.3 broadcast_in_dim.49.clone
  186.6 84.6 %while.29 = (s32[]{:T(128)}, f32[32,128,1,12,128]{1,4,3,0,2:T(8,128)}, f32[32,4,128,1,128]{4,2,0,3,1:T(8,128)}, f32[32,4,128,1,128]{4,2,0,3,1:T(8,128)}, s32[]{:...) while((s32[]{:T(128)}, ...), condition=%wide.region_5.6_spmd, body=%wide.region_4.5_spmd.sunk | while | flops 8122286080 | bytes 221890784 | solution.py:61
  186.6 13.2 %fusion.102 = f32[32,128,128,12]{2,1,3,0:T(8,128)} fusion(bf16[32,128,1,12,128]{4,1,3,0,2:T(8,128)(2,1)} %get-tuple-element.445, bf16[32,4,128,1,128]{4,2,0,3,1:T(8,128)(2,1)} %get-tuple-element.443, s32[]{:T(128)S(6)} %select_n.60), kind=kOutput, calls=%fused_computation.45.clone.1 | convolution fusion | flops 1610612736 | bytes 38797316 | tf_op jit(solution)/shard_map/while/body/bihgd,bjhd->bhgij/dot_general | solution.py:10
  199.8 0.1 broadcast_compare_fusion.5
  199.9 19.9 %fusion.103 = bf16[32,12,128,128]{2,3,1,0:T(8,128)(2,1)} fusion(f32[32,128,128,12]{2,1,3,0:T(8,128)} %fusion.102, f32[32,12,128]{2,1,0:T(8,128)S(1)} %bitcast.253, f32[32,12,128]{2,1,0:T(8,128)S(1)} %bitcast.254, pred[128,128]{0,1:T(8,128)(4,1)S(1)} %broadcast_compare_fusion.5, bf16[32,128,1,12,128]{4,1,3,0,2:T(8,128)(2,1)} %get-tuple-element.448, ...), kind=kOutput, calls=%fused_computation.39.clone.1 | convolution fusion | flops 1648361472 | bytes 51789828 | tf_op jit(solution)/shard_map/while/body/bihgd,bjhd->bhgij/dot_general | solution.py:51
  219.8 22.7 %bitcast_add_fusion.8 = f32[32,128,1,12,128]{1,4,3,0,2:T(8,128)} fusion(f32[32,128,1,12,128]{1,4,3,0,2:T(8,128)} %get-tuple-element.423, bf16[32,12,128,128]{2,3,1,0:T(8,128)(2,1)} %fusion.103, bf16[32,4,128,1,128]{4,2,0,3,1:T(8,128)(2,1)} %get-tuple-element.443, s32[]{:T(128)S(6)} %select_n.60), kind=kOutput, calls=%fused_computation.29.clone.1 | convolution fusion | flops 1616904192 | bytes 63963140 | tf_op jit(solution)/shard_map/while/body/bhgij,bjhd->bihgd/dot_general | solution.py:53
  242.6 12.9 %bitcast_dynamic-update-slice_fusion.4 = f32[32,4,128,1,128]{4,2,0,3,1:T(8,128)} fusion(f32[32,4,128,1,128]{4,2,0,3,1:T(8,128)} %get-tuple-element.424, s32[]{:T(128)S(6)} %select_n.60, bf16[32,12,128,128]{2,3,1,0:T(8,128)(2,1)} %fusion.103, bf16[32,128,1,12,128]{4,1,3,0,2:T(8,128)(2,1)} %get-tuple-element.445), kind=kOutput, calls=%fused_computation.52.clone.1 | convolution fusion | flops 1610612736 | bytes 27262980 | tf_op jit(solution)/shard_map/while/body/bhgij,bihgd->bjhd/dot_general | solution.py:54
  255.5 15.7 %bitcast_dynamic-update-slice_fusion.5 = f32[32,4,128,1,128]{4,2,0,3,1:T(8,128)} fusion(f32[32,4,128,1,128]{4,2,0,3,1:T(8,128)} %get-tuple-element.425, s32[]{:T(128)S(6)} %select_n.60, bf16[32,128,1,12,128]{4,1,3,0,2:T(8,128)(2,1)} %get-tuple-element.448, f32[32,128,128,12]{2,1,3,0:T(8,128)} %fusion.102, f32[32,12,128]{2,1,0:T(8,128)S(1)} %bitcast.255, ...), kind=kOutput, calls=%fused_computation.51.clone.1 | convolution fusion | flops 1635778560 | bytes 40058884 | tf_op jit(solution)/shard_map/while/body/bhgij,bihgd->bjhd/dot_general | solution.py:50
  271.3 0.5 reduce-scatter.9.cloned.1.call-update
  271.8 24.6 %copy.31 = f32[32,128,1,12,128]{4,1,3,0,2:T(8,128)} copy(f32[32,128,1,12,128]{1,4,3,0,2:T(8,128)} %get-tuple-element.122) | data formatting | bytes 50331648 | tf_op jit(solution)/shard_map/while | solution.py:61
  296.5 14.2 %fusion.65 = bf16[32,128,12,128]{3,1,2,0:T(8,128)(2,1)} fusion(f32[32,128,1,12,128]{4,1,3,0,2:T(8,128)} %copy.31), kind=kLoop, calls=%fused_computation.71 | loop fusion | flops 12582912 | bytes 37748736 | tf_op jit(solution)/shard_map/reshape | solution.py:82
  310.7 16.6 %fusion.67 = bf16[32,128,12,128]{3,1,2,0:T(8,128)(2,1)} fusion(f32[32,1,12,128,128]{4,3,2,0,1:T(8,128)} %get-tuple-element.119, f32[32,12,128]{2,1,0:T(8,128)S(1)} %bitcast.246), kind=kLoop, calls=%fused_computation.76 | loop fusion | flops 12582912 | bytes 37945344 | tf_op jit(solution)/shard_map/reshape | solution.py:81
  327.3 421.2 %reduce-scatter.7.cloned.1.call-done = f32[32,1,128,1,128]{4,2,0,3,1:T(8,128)} async-done(((f32[32,4,128,1,128]{4,2,0,3,1:T(8,128)}), f32[32,1,128,1,128]{4,2,0,3,1:T(8,128)}) %reduce-scatter.7.cloned.1.call-update) | async-done | bytes 2097168
  748.5 2.9 fusion.66
  751.4 64.7 %reduce-scatter.9.cloned.1.call-done = f32[32,1,128,1,128]{4,2,0,3,1:T(8,128)} async-done(((f32[32,4,128,1,128]{4,2,0,3,1:T(8,128)}), f32[32,1,128,1,128]{4,2,0,3,1:T(8,128)}) %reduce-scatter.9.cloned.1.call-update) | async-done | bytes 2097168
  816.0 2.7 convert_bitcast_fusion
  (16 shorter events, 0.3 us)
Async XLA Ops:
  7.2 36.7 %all-gather.5.cloned.1.call-start = ((), (), s32[]{:S(2)}) async-start(), calls=%async_computation.2 | async-start | bytes 5242880 | tf_op jit(solution)/shard_map/all_gather | solution.py:75
  7.9 69.0 %all-gather.7.cloned.1.call-start = ((), (), s32[]{:S(2)}) async-start(), calls=%async_computation.3 | async-start | bytes 5242880 | tf_op jit(solution)/shard_map/all_gather | solution.py:76
  8.6 739.9 %reduce-scatter.7.cloned.1.call-start = ((), (), s32[]{:S(2)}) async-start(), calls=%async_computation.4 | async-start | bytes 10485760
  145.9 32.0 %copy-start = (f32[32,1,12,128]{3,2,0,1:T(8,128)}, f32[32,1,12,128]{3,2,0,1:T(8,128)S(1)}, u32[]{:S(2)}) copy-start(f32[32,1,12,128]{3,2,0,1:T(8,128)S(1)} %get-tuple-element.120) | copy-start | bytes 589828
  271.2 544.8 %reduce-scatter.9.cloned.1.call-start = ((), (), s32[]{:S(2)}) async-start(), calls=%async_computation.5 | async-start | bytes 10485760
  296.5 14.2 %copy-start.1 = (f32[32,1,12,128]{3,2,0,1:T(8,128)S(1)}, f32[32,1,12,128]{3,2,0,1:T(8,128)}, u32[]{:S(2)}) copy-start(f32[32,1,12,128]{3,2,0,1:T(8,128)} %copy-done) | copy-start | bytes 589828
Sparse Core Ops, SparseCore 0:
  9.5 34.3 all-gather.4
  45.4 31.4 all-gather.6
  271.4 477.1 reduce-scatter.6
  750.9 65.0 reduce-scatter.8
where the time goes:
time: 826 us; the launch traced here: 825 us
  waiting for transfers between devices  551 us (67%)
  matrix products  125 us (15%)
  other arithmetic  68.8 us (8%)
  local copies, waits for them, and re-layouts  65.9 us (8%)
  between operations  13.8 us (2%)
    unnamed x6, waiting for transfers between devices  488 us
    all_gather x1, waiting for transfers between devices, local_step(): k_all = lax.all_gather(keys, 'ctx', axis=1)  35.2 us
    all_gather x1, waiting for transfers between devices, local_step(): v_all = lax.all_gather(values, 'ctx', axis=1)  28.3 us
    dot_general x1, matrix products, loop_body(): jnp.einsum('bhgij,bjhd->bhgid', weights.astype(jnp.bfloat16), v_blk, pref...  27.4 us
    dot_general x2, matrix products, block_scores(): jnp.einsum('bihgd,bjhd->bhgij', q_heads, k_blk, preferred_element_type=jn...  26.7 us
    while x1, local copies, waits for them, and re-layouts, attend_backward(): return lax.fori_loop(0, dev_idx + 1, loop_body, init_carry)  24.6 us
    dot_general x1, matrix products, loop_body(): jnp.einsum('bhgij,bjhd->bihgd', ds_half, k_blk, preferred_element_type=jn...  22.7 us
    dot_general x1, other arithmetic, attend_backward(): jnp.einsum('bihgd,bihgd->bhgi', do_heads, out_heads, preferred_element_ty...  20.4 us
  transfers between devices with their start and end apart: 4, of which 4 were waited for; matrix products, arithmetic and copies ran while one was open for 8% of the time, Pallas kernels for 0%

commit v1 on v0

v1 whole, which is shorter than its diff:
```python
import functools

import jax
import jax.numpy as jnp
from jax import lax
from jax.experimental import pallas as pl
from jax.experimental.pallas import tpu as pltpu
from jax.sharding import PartitionSpec as P

F32, BF16 = jnp.float32, jnp.bfloat16
LOG2E = 1.4426950408889634
NEG_BIG = -1e30
MESH = pl.DeviceIdType.MESH
RELAY_AHEAD = 2


def dot(a, b):
    return lax.dot_general(a, b, (((1,), (0,)), ((), ())), preferred_element_type=F32)


def remote(src, dst, send_sem, recv_sem, to):
    return pltpu.make_async_remote_copy(src_ref=src, dst_ref=dst, send_sem=send_sem, recv_sem=recv_sem, device_id={"ctx": to}, device_id_type=MESH)


def device_program(me, n_batch, scale, refs):
    (q_hbm, do_hbm, k_hbm, v_hbm, o_hbm, dq_hbm, dk_hbm, dv_hbm,
     kv, acc, part_a, part_b, grads, q_buf, do_buf, o_buf, dq_buf,
     s_0, s_1, p_0, p_1, dp_0, dp_1, ph_0, ph_1, ds_0, ds_1, max_s, inv_s, kt, vt,
     own_sem, kv_sem, kv_send, pa_sem, pb_sem, pa_send, pb_send, red_send,
     q_sem, do_sem, o_sem, dq_sem, dk_sem) = refs
    blocks = me + 1
    width = blocks * 128
    s_buf, p_buf, dp_buf, ph_buf, ds_buf = (s_0, s_1), (p_0, p_1), (dp_0, dp_1), (ph_0, ph_1), (ds_0, ds_1)
    own = pl.ds(me * 128, 128)

    def rows(j):
        return pl.ds(j * 128, 128)

    def own_copy(a, src):
        return pltpu.make_async_copy(src, kv.at[a, :, own], own_sem.at[a])

    def kv_push(a, src, j, b, to, slot):
        return remote(src, kv.at[a, b, rows(j)], kv_send.at[slot, a], kv_sem.at[a, j, b], to)

    def kv_wait(j, b):
        for a in range(2):
            kv_push(a, kv.at[a, b, rows(j)], j, b, me, 0).wait_recv()

    def q_copy(b, slot):
        return pltpu.make_async_copy(q_hbm.at[b], q_buf.at[slot], q_sem.at[slot])

    def do_copy(b, slot):
        return pltpu.make_async_copy(do_hbm.at[b], do_buf.at[slot], do_sem.at[slot])

    def o_copy(b, slot):
        return pltpu.make_async_copy(o_buf.at[slot], o_hbm.at[b], o_sem.at[slot])

    def dq_copy(b, slot):
        return pltpu.make_async_copy(dq_buf.at[slot], dq_hbm.at[b], dq_sem.at[slot])

    def part_push(j, b, dst, send_sem, recv_sem, to):
        return remote(acc.at[b, :, rows(j)], dst.at[b], send_sem, recv_sem.at[b], to)

    first_hop = {0: [], 1: [(0, part_a, pa_send, pa_sem, 0)], 2: [(1, part_a, pa_send, pa_sem, 3)], 3: [(0, part_a, pa_send, pa_sem, 2), (2, part_b, pb_send, pb_sem, 2)]}[me]
    second_hop = {0: None, 1: None, 2: (0, 0), 3: (1, 1)}[me]
    relay = {0: None, 1: None, 2: (0, 3), 3: (1, 2)}[me]

    def relay_block(b):
        j, to = relay
        kv_wait(j, b)
        for a in range(2):
            kv_push(a, kv.at[a, b, rows(j)], j, b, to, 1).start()

    q_copy(0, 0).start()
    do_copy(0, 0).start()
    own_copy(0, k_hbm).start()
    own_copy(1, v_hbm).start()
    direct = {0: (2, 1), 1: (3,), 2: (3,), 3: ()}[me]
    if direct:

        def push_own(b, carry):
            for slot, to in enumerate(direct):
                for a, src in enumerate((k_hbm, v_hbm)):
                    kv_push(a, src.at[b], me, b, to, 2 * slot).start()
            return carry

        lax.fori_loop(0, n_batch, push_own, 0)
    own_copy(0, k_hbm).wait()
    own_copy(1, v_hbm).wait()
    if relay is not None:
        for b in range(RELAY_AHEAD):
            relay_block(b)

    causal_r = lax.broadcasted_iota(jnp.int32, (128, 256), 0)
    causal_c = lax.broadcasted_iota(jnp.int32, (128, 256), 1) & 127

    def pair(ref, slot, x):
        return ref[slot, 2 * x:2 * x + 2].reshape(256, 128)

    def sub_step(sl, one, two, three):
        so = 1 - sl
        if three is not None:
            b3, acc3, slot3, x3 = three
            q3, do3, o3 = pair(q_buf, slot3[0], x3), pair(do_buf, slot3[0], x3), pair(o_buf, slot3[0], x3)
            delta = jnp.sum((do3.astype(F32) * o3.astype(F32)).T, axis=0, keepdims=True)
            inv3 = inv_s[sl, 0:1]
        if two is not None:
            b2, slot2, x2 = two
            max2 = max_s[so, 0:1]
            dot2 = pair(do_buf, slot2[0], x2).T
        if one is not None:
            b1, slot1, x1 = one
            qt1 = pair(q_buf, slot1[0], x1).T
        max8 = sum8 = None
        for j in range(blocks):
            r = slice(j * 128, j * 128 + 128)
            if two is not None:
                p = jnp.exp2((s_buf[so][r] - max2) * (scale * LOG2E))
                p_buf[so][r] = p
                ph_buf[so][r] = p.astype(BF16)
                part = jnp.sum(p.reshape(16, 8, 256), axis=0)
                sum8 = part if sum8 is None else sum8 + part
            if one is not None:
                st = dot(kv[0, b1, r], qt1)
                if j == blocks - 1:
                    st = jnp.where(causal_r <= causal_c, st, NEG_BIG)
                s_buf[sl][r] = st
                part = jnp.max(st.reshape(16, 8, 256), axis=0)
                max8 = part if max8 is None else jnp.maximum(max8, part)
        if two is not None:
            inv = 1.0 / jnp.sum(sum8, axis=0, keepdims=True)
            inv_s[so, 0:1] = inv
            ot = (dot(vt[slot2[1], :, :width], ph_buf[so][:width]) * inv).astype(BF16)
            o_buf[slot2[0], 2 * x2:2 * x2 + 2] = ot.T.reshape(2, 128, 128)
        if one is not None:
            max_s[sl, 0:1] = jnp.max(max8, axis=0, keepdims=True)
        for j in range(blocks):
            r = slice(j * 128, j * 128 + 128)
            if three is not None:
                pb = p_buf[sl][r] * inv3
                ds = (pb * (dp_buf[sl][r] - delta)).astype(BF16)
                ds_buf[sl][r] = ds
                dv = dot(pb.astype(BF16), do3)
                dk = dot(ds, q3)
                if x3 == 0:
                    acc[acc3, 0, r] = dk
                    acc[acc3, 1, r] = dv
                else:
                    acc[acc3, 0, r] += dk
                    acc[acc3, 1, r] += dv
            if two is not None:
                dp_buf[so][r] = dot(kv[1, b2, r], dot2)
        if three is not None:
            dq = (dot(kt[slot3[1], :, :width], ds_buf[sl][:width]) * scale).astype(BF16)
            dq_buf[slot3[0], 2 * x3:2 * x3 + 2] = dq.T.reshape(2, 128, 128)

    def reduce_part(b):
        j, _ = second_hop
        part_push(j, b, part_a, pa_send, pa_sem, me).wait_recv()
        acc[b, :, rows(j)] += part_a[b]

    def send_reduced(b):
        j, to = second_hop
        part_push(j, b, part_b, red_send, pb_sem, to).start()

    def finish(b, slot):
        o_copy(b, slot).start()
        dq_copy(b, slot).start()
        for hop in first_hop:
            part_push(hop[0], b, hop[1], hop[2], hop[3], hop[4]).start()

    def step(b, carry):
        cur, prev = lax.rem(b, 3), lax.rem(b + 2, 3)
        tcur, tprev = lax.rem(b, 2), lax.rem(b + 1, 2)
        b_prev = jnp.maximum(b - 1, 0)
        acc_prev = jnp.where(b == 0, n_batch, b - 1)

        @pl.when(b + 1 < n_batch)
        def _():
            nxt = lax.rem(b + 1, 3)
            q_copy(b + 1, nxt).start()
            do_copy(b + 1, nxt).start()

        @pl.when(b >= 3)
        def _():
            o_copy(b - 3, cur).wait()
            dq_copy(b - 3, cur).wait()

        if relay is not None:

            @pl.when(b + RELAY_AHEAD < n_batch)
            def _():
                relay_block(b + RELAY_AHEAD)

        for j in range(me):
            if relay is None or j != relay[0]:
                kv_wait(j, b)
        q_copy(b, cur).wait()
        do_copy(b, cur).wait()
        kt[tcur, :, :width] = kv[0, b, :width].T
        vt[tcur, :, :width] = kv[1, b, :width].T
        for x in range(6):
            two = (b_prev, (prev, tprev), 5) if x == 0 else (b, (cur, tcur), x - 1)
            three = (b_prev, acc_prev, (prev, tprev), x + 4) if x < 2 else (b, b, (cur, tcur), x - 2)
            sub_step(x % 2, (b, (cur, tcur), x), two, three)

        if second_hop is not None:

            @pl.when(b >= 2)
            def _():
                reduce_part(b - 2)

        @pl.when(b >= 1)
        def _():
            finish(b - 1, prev)

        if second_hop is not None:

            @pl.when(b >= 2)
            def _():
                send_reduced(b - 2)

        return carry

    lax.fori_loop(0, n_batch, step, 0)

    last = n_batch - 1
    ls, lt = last % 3, last % 2
    sub_step(0, None, (last, (ls, lt), 5), (last, last, (ls, lt), 4))
    sub_step(1, None, None, (last, last, (ls, lt), 5))
    if second_hop is not None:
        reduce_part(last - 1)
    finish(last, ls)
    if second_hop is not None:
        send_reduced(last - 1)
        reduce_part(last)
        send_reduced(last)

    def finalize(b, carry):
        total = acc[b, :, own]
        if me == 0:
            part_push(0, b, part_a, pa_send, pa_sem, me).wait_recv()
            total = total + part_a[b]
        if me < 3:
            part_push(0, b, part_b, pb_send, pb_sem, me).wait_recv()
            total = total + part_b[b]
        grads[b, 0] = (total[0] * scale).astype(BF16)
        grads[b, 1] = total[1].astype(BF16)
        pltpu.make_async_copy(grads.at[b, 0], dk_hbm.at[b], dk_sem.at[0]).start()
        pltpu.make_async_copy(grads.at[b, 1], dv_hbm.at[b], dk_sem.at[1]).start()
        return carry

    lax.fori_loop(0, n_batch, finalize, 0)

    for b in range(n_batch - 3, n_batch):
        o_copy(b, b % 3).wait()
        dq_copy(b, b % 3).wait()
    pltpu.make_async_copy(grads.at[:, 0], dk_hbm, dk_sem.at[0]).wait()
    pltpu.make_async_copy(grads.at[:, 1], dv_hbm, dk_sem.at[1]).wait()
    for slot in range(len(direct)):
        for a, src in enumerate((k_hbm, v_hbm)):
            remote(src, kv.at[a, :, own], kv_send.at[2 * slot, a], kv_sem.at[a, 0, 0], me).wait_send()
    if relay is not None:
        for a in range(2):
            remote(kv.at[a, :, rows(relay[0])], kv.at[a, :, own], kv_send.at[1, a], kv_sem.at[a, 0, 0], me).wait_send()
    every = pl.ds(0, n_batch)
    for j, dst, send_sem, _, _ in first_hop:
        remote(acc.at[every, :, rows(j)], dst, send_sem, pa_sem.at[0], me).wait_send()
    if second_hop is not None:
        remote(acc.at[every, :, rows(second_hop[0])], part_b, red_send, pa_sem.at[0], me).wait_send()


def kernel(n_ctx, n_batch, scale, *refs):
    me = lax.axis_index("ctx")
    barrier = pltpu.get_barrier_semaphore()
    for step in range(1, n_ctx):
        pl.semaphore_signal(barrier, inc=1, device_id={"ctx": lax.rem(me + step, n_ctx)}, device_id_type=MESH)
    pl.semaphore_wait(barrier, n_ctx - 1)
    for i in range(n_ctx):
        pl.when(me == i)(functools.partial(device_program, i, n_batch, scale, refs))


def solution(mesh):
    part_spec = P("dp", "ctx")
    n_ctx = mesh.shape["ctx"]

    def local_step(queries, keys, values, grad_out):
        n_batch, c_len, n_q, d_head = queries.shape
        heads = (0, 2, 1, 3)
        q, do = jnp.transpose(queries, heads), jnp.transpose(grad_out, heads)
        k, v = keys.reshape(n_batch, c_len, d_head), values.reshape(n_batch, c_len, d_head)
        width = n_ctx * c_len
        vmem, dma = pltpu.VMEM, pltpu.SemaphoreType.DMA
        scratch = [
            vmem((2, n_batch, width, d_head), BF16),
            vmem((n_batch + 1, 2, width, d_head), F32),
            vmem((n_batch, 2, c_len, d_head), F32),
            vmem((n_batch, 2, c_len, d_head), F32),
            vmem((n_batch, 2, c_len, d_head), BF16),
        ]
        scratch += [vmem((3, n_q, c_len, d_head), BF16)] * 4
        scratch += [vmem((width, 256), F32)] * 6 + [vmem((width, 256), BF16)] * 4
        scratch += [vmem((2, 8, 256), F32)] * 2 + [vmem((2, d_head, width), BF16)] * 2
        scratch += [dma((2,)), dma((2, n_ctx, n_batch)), dma((3, 2)), dma((n_batch,)), dma((n_batch,)), dma, dma, dma]
        scratch += [dma((3,))] * 4 + [dma((2,))]
        hbm = pl.BlockSpec(memory_space=pl.ANY)
        out_q, out_k = jax.ShapeDtypeStruct(q.shape, BF16), jax.ShapeDtypeStruct(k.shape, BF16)
        out, grad_q, grad_k, grad_v = pl.pallas_call(
            functools.partial(kernel, n_ctx, n_batch, d_head ** -0.5),
            out_shape=[out_q, out_q, out_k, out_k],
            in_specs=[hbm] * 4,
            out_specs=[hbm] * 4,
            scratch_shapes=scratch,
            compiler_params=pltpu.CompilerParams(collective_id=0, has_side_effects=True, vmem_limit_bytes=62 * 2 ** 20),
        )(q, do, k, v)
        return jnp.transpose(out, heads), jnp.transpose(grad_q, heads), grad_k.reshape(keys.shape), grad_v.reshape(values.shape)

    return jax.shard_map(local_step, mesh=mesh, in_specs=(part_spec,) * 4, out_specs=(part_spec,) * 4, check_vma=False)
```

time: 826 us -> 142 us (0.17)
  waiting for transfers between devices: 551 us -> 0 us
  matrix products: 125 us -> 0 us
  Pallas kernels: 0 us -> 121 us
  other arithmetic: 68.8 us -> 0 us
  local copies, waits for them, and re-layouts: 65.9 us -> 19.5 us
  between operations: 13.8 us -> 0.65 us
    unnamed x6 -> x0, waiting for transfers between devices: 488 us -> none
    dot_general x7 -> x0, matrix products: 125 us -> none  [the longest x1 27.4 us: loop_body(): jnp.einsum('bhgij,bjhd->bhgid', weights.astype(jnp.bfloat16), v_blk, pref...]
    pallas_call x0 -> x1, Pallas kernels: none -> 121 us  [local_step(): pl.pallas_call(functools.partial(kernel, n_ctx, n_batch, d_head ** (-0.5)...]
    all_gather x2 -> x0, waiting for transfers between devices: 63.4 us -> none  [the longest x1 35.2 us: local_step(): k_all = lax.all_gather(keys, 'ctx', axis=1)]
    while x4 -> x0, local copies, waits for them, and re-layouts: 34.2 us -> none  [the longest x1 24.6 us: attend_backward(): return lax.fori_loop(0, dev_idx + 1, loop_body, init_carry)]
    broadcast_in_dim x6 -> x0, local copies, waits for them, and re-layouts: 31.7 us -> none  [the longest x1 11.5 us: attend_forward(): jnp.zeros(stat_shape + (d_head,), jnp.float32)]
    reshape x2 -> x0, other arithmetic: 30.9 us -> none  [the longest x1 16.6 us: local_step(): attn_out = out_heads.reshape(n_batch, c_len, n_q, d_head)]
    dot_general x1 -> x0, other arithmetic: 20.4 us -> none  [attend_backward(): jnp.einsum('bihgd,bihgd->bhgi', do_heads, out_heads, preferred_element_ty...]
  transfers between devices with their start and end apart: 4 -> 0, of which waited for: 4 -> 0; matrix products, arithmetic and copies ran while one was open for 8% -> 0% of each run, Pallas kernels for 0% -> 0%
where the time goes in v1:
time: 142 us
  Pallas kernels  121 us (85%)
  local copies, waits for them, and re-layouts  19.5 us (14%)
    pallas_call x1, Pallas kernels, local_step(): pl.pallas_call(functools.partial(kernel, n_ctx, n_batch, d_head ** (-0.5)...  121 us
    unnamed x10, local copies, waits for them, and re-layouts  19.5 us

profile of v1, /device:TPU:0, one launch (start us, length us, event | category | flops | bytes accessed | tf_op | source)
XLA Modules:
  0.0 141.5 jit_solution(3369298244575422135)
XLA Ops:
  0.6 121.4 %shard_map.75 = (bf16[32,12,128,128]{3,2,1,0:T(8,128)(2,1)}, bf16[32,12,128,128]{3,2,1,0:T(8,128)(2,1)}, bf16[32,128,128]{2,1,0:T(8,128)(2,1)}, bf16[32,128,128]{2,1,0:T(8,128)(2,1)}) custom-call(bf16[32,12,128,128]{3,2,1,0:T(8,128)(2,1)} %bitcast.14, bf16[32,12,128,128]{3,2,1,0:T(8,128)(2,1)} %bitcast.15, bf16[32,128,128]{2,1,0:T(8,128)(2,1)} %bitcast.18, ...), custom_call_target="tpu_custom_call" | custom-call | tf_op jit(solution)/shard_map/pallas_call | solution.py:308
  122.0 0.0 copy-start
  122.0 12.7 %copy.14 = bf16[32,128,12,128]{3,1,2,0:T(8,128)(2,1)} copy(bf16[32,128,12,128]{3,1,2,0:T(8,128)(2,1)} %bitcast.13) | data formatting | bytes 25165824
  134.7 0.0 copy-done
  134.7 0.0 copy-start.2
  134.7 0.0 copy-start.1
  134.7 4.9 %copy.15 = bf16[32,128,12,128]{3,1,2,0:T(8,128)(2,1)} copy(bf16[32,128,12,128]{3,1,2,0:T(8,128)(2,1)S(1)} %bitcast.12) | data formatting | bytes 25165824
  139.6 0.0 copy-done.2
  139.6 1.0 copy.16
  140.6 0.0 copy-done.1
  140.6 1.0 copy.17
Async XLA Ops:
  122.0 12.7 %copy-start = (bf16[32,12,128,128]{3,2,1,0:T(8,128)(2,1)S(1)}, bf16[32,12,128,128]{3,2,1,0:T(8,128)(2,1)}, u32[]{:S(2)}) copy-start(bf16[32,12,128,128]{3,2,1,0:T(8,128)(2,1)} %get-tuple-element.9) | copy-start | bytes 37748740
  134.7 4.9 %copy-start.2 = (bf16[32,128,128]{2,1,0:T(8,128)(2,1)S(1)}, bf16[32,128,128]{2,1,0:T(8,128)(2,1)}, u32[]{:S(2)}) copy-start(bf16[32,128,128]{2,1,0:T(8,128)(2,1)} %get-tuple-element.10) | copy-start | bytes 3145732
  134.7 5.9 %copy-start.1 = (bf16[32,128,128]{2,1,0:T(8,128)(2,1)S(1)}, bf16[32,128,128]{2,1,0:T(8,128)(2,1)}, u32[]{:S(2)}) copy-start(bf16[32,128,128]{2,1,0:T(8,128)(2,1)} %get-tuple-element.11) | copy-start | bytes 3145732

commit v2 on v1

--- a/solution.py
+++ b/solution.py
@@ -11,7 +11,8 @@
 LOG2E = 1.4426950408889634
 NEG_BIG = -1e30
 MESH = pl.DeviceIdType.MESH
-RELAY_AHEAD = 2
+RELAY_AHEAD = 1
+PIECE = 32
 
 
 def dot(a, b):
@@ -25,12 +26,12 @@
 def device_program(me, n_batch, scale, refs):
     (q_hbm, do_hbm, k_hbm, v_hbm, o_hbm, dq_hbm, dk_hbm, dv_hbm,
      kv, acc, part_a, part_b, grads, q_buf, do_buf, o_buf, dq_buf,
-     s_0, s_1, p_0, p_1, dp_0, dp_1, ph_0, ph_1, ds_0, ds_1, max_s, inv_s, kt, vt,
+     s_0, s_1, p_0, p_1, p_2, dp_0, dp_1, ph_0, ph_1, ds_0, ds_1, pb_buf, max_s, inv_s, delta_s, kt, vt,
      own_sem, kv_sem, kv_send, pa_sem, pb_sem, pa_send, pb_send, red_send,
      q_sem, do_sem, o_sem, dq_sem, dk_sem) = refs
     blocks = me + 1
     width = blocks * 128
-    s_buf, p_buf, dp_buf, ph_buf, ds_buf = (s_0, s_1), (p_0, p_1), (dp_0, dp_1), (ph_0, ph_1), (ds_0, ds_1)
+    s_buf, p_buf, dp_buf, ph_buf, ds_buf = (s_0, s_1), (p_0, p_1, p_2), (dp_0, dp_1), (ph_0, ph_1), (ds_0, ds_1)
     own = pl.ds(me * 128, 128)
 
     def rows(j):
@@ -97,62 +98,63 @@
     def pair(ref, slot, x):
         return ref[slot, 2 * x:2 * x + 2].reshape(256, 128)
 
-    def sub_step(sl, one, two, three):
-        so = 1 - sl
-        if three is not None:
-            b3, acc3, slot3, x3 = three
-            q3, do3, o3 = pair(q_buf, slot3[0], x3), pair(do_buf, slot3[0], x3), pair(o_buf, slot3[0], x3)
-            delta = jnp.sum((do3.astype(F32) * o3.astype(F32)).T, axis=0, keepdims=True)
-            inv3 = inv_s[sl, 0:1]
-        if two is not None:
-            b2, slot2, x2 = two
-            max2 = max_s[so, 0:1]
-            dot2 = pair(do_buf, slot2[0], x2).T
-        if one is not None:
-            b1, slot1, x1 = one
-            qt1 = pair(q_buf, slot1[0], x1).T
+    def sub_step(x, stages):
+        par = [(x - k) % 2 for k in range(5)]
+        tri = [(x - k) % 3 for k in range(5)]
+        s0, s1, s2, s3, s4 = stages
+        if s0 is not None:
+            qt0 = pair(q_buf, s0[2], s0[4]).T
+        if s2 is not None:
+            dot2 = pair(do_buf, s2[2], s2[4]).T
+        if s1 is not None:
+            max1 = max_s[par[1], 0:1]
+        if s3 is not None:
+            q3, do3 = pair(q_buf, s3[2], s3[4]), pair(do_buf, s3[2], s3[4])
+            inv3, delta3 = inv_s[tri[3], 0:1], delta_s[par[3], 0:1]
         max8 = sum8 = None
         for j in range(blocks):
             r = slice(j * 128, j * 128 + 128)
-            if two is not None:
-                p = jnp.exp2((s_buf[so][r] - max2) * (scale * LOG2E))
-                p_buf[so][r] = p
-                ph_buf[so][r] = p.astype(BF16)
-                part = jnp.sum(p.reshape(16, 8, 256), axis=0)
-                sum8 = part if sum8 is None else sum8 + part
-            if one is not None:
-                st = dot(kv[0, b1, r], qt1)
+            pieces = [slice(y, y + PIECE) for y in range(j * 128, j * 128 + 128, PIECE)]
+            if j == 0 and s2 is not None:
+                ot = (dot(vt[s2[3], :, :width], ph_buf[par[2]][:width]) * inv_s[tri[2], 0:1]).astype(BF16)
+                o_buf[s2[2], 2 * s2[4]:2 * s2[4] + 2] = ot.T.reshape(2, 128, 128)
+                delta_s[par[2], 0:1] = jnp.sum(dot2.astype(F32) * ot.astype(F32), axis=0, keepdims=True)
+            if j == min(1, blocks - 1) and s4 is not None:
+                dq = (dot(kt[s4[3], :, :width], ds_buf[par[4]][:width]) * scale).astype(BF16)
+                dq_buf[s4[2], 2 * s4[4]:2 * s4[4] + 2] = dq.T.reshape(2, 128, 128)
+            if s3 is not None:
+                for y in pieces:
+                    pb = p_buf[tri[3]][y] * inv3
+                    ds_buf[par[3]][y] = (pb * (dp_buf[par[3]][y] - delta3)).astype(BF16)
+                    pb_buf[y] = pb.astype(BF16)
+                dv = dot(pb_buf[r], do3)
+                dk = dot(ds_buf[par[3]][r], q3)
+                if s3[4] == 0:
+                    acc[s3[1], 0, r] = dk
+                    acc[s3[1], 1, r] = dv
+                else:
+                    acc[s3[1], 0, r] += dk
+                    acc[s3[1], 1, r] += dv
+            if s0 is not None:
+                st = dot(kv[0, s0[0], r], qt0)
                 if j == blocks - 1:
                     st = jnp.where(causal_r <= causal_c, st, NEG_BIG)
-                s_buf[sl][r] = st
+                s_buf[par[0]][r] = st
                 part = jnp.max(st.reshape(16, 8, 256), axis=0)
                 max8 = part if max8 is None else jnp.maximum(max8, part)
-        if two is not None:
-            inv = 1.0 / jnp.sum(sum8, axis=0, keepdims=True)
-            inv_s[so, 0:1] = inv
-            ot = (dot(vt[slot2[1], :, :width], ph_buf[so][:width]) * inv).astype(BF16)
-            o_buf[slot2[0], 2 * x2:2 * x2 + 2] = ot.T.reshape(2, 128, 128)
-        if one is not None:
-            max_s[sl, 0:1] = jnp.max(max8, axis=0, keepdims=True)
-        for j in range(blocks):
-            r = slice(j * 128, j * 128 + 128)
-            if three is not None:
-                pb = p_buf[sl][r] * inv3
-                ds = (pb * (dp_buf[sl][r] - delta)).astype(BF16)
-                ds_buf[sl][r] = ds
-                dv = dot(pb.astype(BF16), do3)
-                dk = dot(ds, q3)
-                if x3 == 0:
-                    acc[acc3, 0, r] = dk
-                    acc[acc3, 1, r] = dv
-                else:
-                    acc[acc3, 0, r] += dk
-                    acc[acc3, 1, r] += dv
-            if two is not None:
-                dp_buf[so][r] = dot(kv[1, b2, r], dot2)
-        if three is not None:
-            dq = (dot(kt[slot3[1], :, :width], ds_buf[sl][:width]) * scale).astype(BF16)
-            dq_buf[slot3[0], 2 * x3:2 * x3 + 2] = dq.T.reshape(2, 128, 128)
+            if s1 is not None:
+                for y in pieces:
+                    p = jnp.exp2((s_buf[par[1]][y] - max1) * (scale * LOG2E))
+                    p_buf[tri[1]][y] = p
+                    ph_buf[par[1]][y] = p.astype(BF16)
+                    part = jnp.sum(p.reshape(PIECE // 8, 8, 256), axis=0)
+                    sum8 = part if sum8 is None else sum8 + part
+            if s2 is not None:
+                dp_buf[par[2]][r] = dot(kv[1, s2[0], r], dot2)
+        if s1 is not None:
+            inv_s[tri[1], 0:1] = 1.0 / jnp.sum(sum8, axis=0, keepdims=True)
+        if s0 is not None:
+            max_s[par[0], 0:1] = jnp.max(max8, axis=0, keepdims=True)
 
     def reduce_part(b):
         j, _ = second_hop
@@ -163,11 +165,11 @@
         j, to = second_hop
         part_push(j, b, part_b, red_send, pb_sem, to).start()
 
-    def finish(b, slot):
-        o_copy(b, slot).start()
-        dq_copy(b, slot).start()
-        for hop in first_hop:
-            part_push(hop[0], b, hop[1], hop[2], hop[3], hop[4]).start()
+    def send_parts(b):
+        for j, dst, send_sem, recv_sem, to in first_hop:
+            part_push(j, b, dst, send_sem, recv_sem, to).start()
+
+    lag = 1 if me == 3 else 3
 
     def step(b, carry):
         cur, prev = lax.rem(b, 3), lax.rem(b + 2, 3)
@@ -200,41 +202,41 @@
         kt[tcur, :, :width] = kv[0, b, :width].T
         vt[tcur, :, :width] = kv[1, b, :width].T
         for x in range(6):
-            two = (b_prev, (prev, tprev), 5) if x == 0 else (b, (cur, tcur), x - 1)
-            three = (b_prev, acc_prev, (prev, tprev), x + 4) if x < 2 else (b, b, (cur, tcur), x - 2)
-            sub_step(x % 2, (b, (cur, tcur), x), two, three)
-
+            here = (b, b, cur, tcur)
+            before = (b_prev, acc_prev, prev, tprev)
+            sub_step(x, [here + (x - k,) if x >= k else before + (x - k + 6,) for k in range(5)])
+        pl.when(b >= 1)(lambda: send_parts(b - 1))
         if second_hop is not None:
-
-            @pl.when(b >= 2)
-            def _():
-                reduce_part(b - 2)
+            pl.when(b >= lag)(lambda: reduce_part(b - lag))
 
         @pl.when(b >= 1)
         def _():
-            finish(b - 1, prev)
+            o_copy(b - 1, prev).start()
+            dq_copy(b - 1, prev).start()
 
         if second_hop is not None:
-
-            @pl.when(b >= 2)
-            def _():
-                send_reduced(b - 2)
-
+            pl.when(b >= lag)(lambda: send_reduced(b - lag))
         return carry
 
     lax.fori_loop(0, n_batch, step, 0)
 
     last = n_batch - 1
-    ls, lt = last % 3, last % 2
-    sub_step(0, None, (last, (ls, lt), 5), (last, last, (ls, lt), 4))
-    sub_step(1, None, None, (last, last, (ls, lt), 5))
-    if second_hop is not None:
-        reduce_part(last - 1)
-    finish(last, ls)
-    if second_hop is not None:
-        send_reduced(last - 1)
+    ls = last % 3
+    end = (last, last, ls, last % 2)
+    for x in range(3):
+        sub_step(x, [end + (x - k + 6,) if k > x else None for k in range(5)])
+    send_parts(last)
+    if me == 3:
         reduce_part(last)
+    sub_step(3, [None, None, None, None, end + (5,)])
+    if me == 3:
         send_reduced(last)
+    o_copy(last, ls).start()
+    dq_copy(last, ls).start()
+    if me == 2:
+        for b in range(n_batch - lag, n_batch):
+            reduce_part(b)
+            send_reduced(b)
 
     def finalize(b, carry):
         total = acc[b, :, own]
@@ -299,8 +301,8 @@
             vmem((n_batch, 2, c_len, d_head), BF16),
         ]
         scratch += [vmem((3, n_q, c_len, d_head), BF16)] * 4
-        scratch += [vmem((width, 256), F32)] * 6 + [vmem((width, 256), BF16)] * 4
-        scratch += [vmem((2, 8, 256), F32)] * 2 + [vmem((2, d_head, width), BF16)] * 2
+        scratch += [vmem((width, 256), F32)] * 7 + [vmem((width, 256), BF16)] * 5
+        scratch += [vmem((2, 8, 256), F32), vmem((3, 8, 256), F32), vmem((2, 8, 256), F32)] + [vmem((2, d_head, width), BF16)] * 2
         scratch += [dma((2,)), dma((2, n_ctx, n_batch)), dma((3, 2)), dma((n_batch,)), dma((n_batch,)), dma, dma, dma]
         scratch += [dma((3,))] * 4 + [dma((2,))]
         hbm = pl.BlockSpec(memory_space=pl.ANY)

time: 142 us -> 135 us (0.951)
  Pallas kernels: 121 us -> 114 us
    pallas_call x1, Pallas kernels: 121 us -> 114 us  [local_step(): pl.pallas_call(functools.partial(kernel, n_ctx, n_batch, d_head ** (-0.5)...]
where the time goes in v2:
time: 135 us; the launch traced here: 134 us
  Pallas kernels  114 us (84%)
  local copies, waits for them, and re-layouts  19.5 us (14%)
    pallas_call x1, Pallas kernels, local_step(): pl.pallas_call(functools.partial(kernel, n_ctx, n_batch, d_head ** (-0.5)...  114 us
    unnamed x10, local copies, waits for them, and re-layouts  19.5 us

profile of v2, /device:TPU:0, one launch (start us, length us, event | category | flops | bytes accessed | tf_op | source)
XLA Modules:
  0.0 133.7 jit_solution(11562531672195833785)
XLA Ops:
  0.6 113.6 %shard_map.75 = (bf16[32,12,128,128]{3,2,1,0:T(8,128)(2,1)}, bf16[32,12,128,128]{3,2,1,0:T(8,128)(2,1)}, bf16[32,128,128]{2,1,0:T(8,128)(2,1)}, bf16[32,128,128]{2,1,0:T(8,128)(2,1)}) custom-call(bf16[32,12,128,128]{3,2,1,0:T(8,128)(2,1)} %bitcast.14, bf16[32,12,128,128]{3,2,1,0:T(8,128)(2,1)} %bitcast.15, bf16[32,128,128]{2,1,0:T(8,128)(2,1)} %bitcast.18, ...), custom_call_target="tpu_custom_call" | custom-call | tf_op jit(solution)/shard_map/pallas_call | solution.py:310
  114.2 0.0 copy-start
  114.2 12.7 %copy.14 = bf16[32,128,12,128]{3,1,2,0:T(8,128)(2,1)} copy(bf16[32,128,12,128]{3,1,2,0:T(8,128)(2,1)} %bitcast.13) | data formatting | bytes 25165824
  126.9 0.0 copy-done
  126.9 0.0 copy-start.2
  126.9 0.0 copy-start.1
  126.9 4.9 %copy.15 = bf16[32,128,12,128]{3,1,2,0:T(8,128)(2,1)} copy(bf16[32,128,12,128]{3,1,2,0:T(8,128)(2,1)S(1)} %bitcast.12) | data formatting | bytes 25165824
  131.8 0.0 copy-done.2
  131.8 1.0 copy.16
  132.8 0.0 copy-done.1
  132.8 1.0 copy.17
Async XLA Ops:
  114.2 12.7 %copy-start = (bf16[32,12,128,128]{3,2,1,0:T(8,128)(2,1)S(1)}, bf16[32,12,128,128]{3,2,1,0:T(8,128)(2,1)}, u32[]{:S(2)}) copy-start(bf16[32,12,128,128]{3,2,1,0:T(8,128)(2,1)} %get-tuple-element.9) | copy-start | bytes 37748740
  126.9 4.9 %copy-start.2 = (bf16[32,128,128]{2,1,0:T(8,128)(2,1)S(1)}, bf16[32,128,128]{2,1,0:T(8,128)(2,1)}, u32[]{:S(2)}) copy-start(bf16[32,128,128]{2,1,0:T(8,128)(2,1)} %get-tuple-element.10) | copy-start | bytes 3145732
  126.9 5.9 %copy-start.1 = (bf16[32,128,128]{2,1,0:T(8,128)(2,1)S(1)}, bf16[32,128,128]{2,1,0:T(8,128)(2,1)}, u32[]{:S(2)}) copy-start(bf16[32,128,128]{2,1,0:T(8,128)(2,1)} %get-tuple-element.11) | copy-start | bytes 3145732

commit v3 on v2

--- a/solution.py
+++ b/solution.py
@@ -12,6 +12,8 @@
 NEG_BIG = -1e30
 MESH = pl.DeviceIdType.MESH
 RELAY_AHEAD = 1
+RING = 8
+CHUNKS = 4
 PIECE = 32
 
 
@@ -24,11 +26,11 @@
 
 
 def device_program(me, n_batch, scale, refs):
-    (q_hbm, do_hbm, k_hbm, v_hbm, o_hbm, dq_hbm, dk_hbm, dv_hbm,
-     kv, acc, part_a, part_b, grads, q_buf, do_buf, o_buf, dq_buf,
+    (q_hbm, do_hbm, k_hbm, v_hbm, o_out, dq_out, dk_out, dv_out,
+     kv, own_acc, ring, part_a, part_b, q_buf, do_buf,
      s_0, s_1, p_0, p_1, p_2, dp_0, dp_1, ph_0, ph_1, ds_0, ds_1, pb_buf, max_s, inv_s, delta_s, kt, vt,
      own_sem, kv_sem, kv_send, pa_sem, pb_sem, pa_send, pb_send, red_send,
-     q_sem, do_sem, o_sem, dq_sem, dk_sem) = refs
+     q_sem, do_sem) = refs
     blocks = me + 1
     width = blocks * 128
     s_buf, p_buf, dp_buf, ph_buf, ds_buf = (s_0, s_1), (p_0, p_1, p_2), (dp_0, dp_1), (ph_0, ph_1), (ds_0, ds_1)
@@ -53,14 +55,9 @@
     def do_copy(b, slot):
         return pltpu.make_async_copy(do_hbm.at[b], do_buf.at[slot], do_sem.at[slot])
 
-    def o_copy(b, slot):
-        return pltpu.make_async_copy(o_buf.at[slot], o_hbm.at[b], o_sem.at[slot])
-
-    def dq_copy(b, slot):
-        return pltpu.make_async_copy(dq_buf.at[slot], dq_hbm.at[b], dq_sem.at[slot])
-
     def part_push(j, b, dst, send_sem, recv_sem, to):
-        return remote(acc.at[b, :, rows(j)], dst.at[b], send_sem, recv_sem.at[b], to)
+        slot = lax.rem(b, RING) if not isinstance(b, int) else b % RING
+        return remote(ring.at[slot, :, rows(j)], dst.at[b], send_sem.at[slot], recv_sem.at[b], to)
 
     first_hop = {0: [], 1: [(0, part_a, pa_send, pa_sem, 0)], 2: [(1, part_a, pa_send, pa_sem, 3)], 3: [(0, part_a, pa_send, pa_sem, 2), (2, part_b, pb_send, pb_sem, 2)]}[me]
     second_hop = {0: None, 1: None, 2: (0, 0), 3: (1, 1)}[me]
@@ -103,25 +100,25 @@
         tri = [(x - k) % 3 for k in range(5)]
         s0, s1, s2, s3, s4 = stages
         if s0 is not None:
-            qt0 = pair(q_buf, s0[2], s0[4]).T
+            qt0 = pair(q_buf, s0[3], s0[5]).T
         if s2 is not None:
-            dot2 = pair(do_buf, s2[2], s2[4]).T
+            dot2 = pair(do_buf, s2[3], s2[5]).T
         if s1 is not None:
             max1 = max_s[par[1], 0:1]
         if s3 is not None:
-            q3, do3 = pair(q_buf, s3[2], s3[4]), pair(do_buf, s3[2], s3[4])
+            q3, do3 = pair(q_buf, s3[3], s3[5]), pair(do_buf, s3[3], s3[5])
             inv3, delta3 = inv_s[tri[3], 0:1], delta_s[par[3], 0:1]
         max8 = sum8 = None
         for j in range(blocks):
             r = slice(j * 128, j * 128 + 128)
             pieces = [slice(y, y + PIECE) for y in range(j * 128, j * 128 + 128, PIECE)]
             if j == 0 and s2 is not None:
-                ot = (dot(vt[s2[3], :, :width], ph_buf[par[2]][:width]) * inv_s[tri[2], 0:1]).astype(BF16)
-                o_buf[s2[2], 2 * s2[4]:2 * s2[4] + 2] = ot.T.reshape(2, 128, 128)
+                ot = (dot(vt[s2[4], :, :width], ph_buf[par[2]][:width]) * inv_s[tri[2], 0:1]).astype(BF16)
+                o_out[s2[0], 2 * s2[5]:2 * s2[5] + 2] = ot.T.reshape(2, 128, 128)
                 delta_s[par[2], 0:1] = jnp.sum(dot2.astype(F32) * ot.astype(F32), axis=0, keepdims=True)
             if j == min(1, blocks - 1) and s4 is not None:
-                dq = (dot(kt[s4[3], :, :width], ds_buf[par[4]][:width]) * scale).astype(BF16)
-                dq_buf[s4[2], 2 * s4[4]:2 * s4[4] + 2] = dq.T.reshape(2, 128, 128)
+                dq = (dot(kt[s4[4], :, :width], ds_buf[par[4]][:width]) * scale).astype(BF16)
+                dq_out[s4[0], 2 * s4[5]:2 * s4[5] + 2] = dq.T.reshape(2, 128, 128)
             if s3 is not None:
                 for y in pieces:
                     pb = p_buf[tri[3]][y] * inv3
@@ -129,12 +126,9 @@
                     pb_buf[y] = pb.astype(BF16)
                 dv = dot(pb_buf[r], do3)
                 dk = dot(ds_buf[par[3]][r], q3)
-                if s3[4] == 0:
-                    acc[s3[1], 0, r] = dk
-                    acc[s3[1], 1, r] = dv
-                else:
-                    acc[s3[1], 0, r] += dk
-                    acc[s3[1], 1, r] += dv
+                for w, part in enumerate((dk, dv)):
+                    dst, at = (own_acc, (s3[1], w)) if j == me else (ring, (s3[2], w, r))
+                    dst[at] = part if s3[5] == 0 else dst[at] + part
             if s0 is not None:
                 st = dot(kv[0, s0[0], r], qt0)
                 if j == blocks - 1:
@@ -159,7 +153,8 @@
     def reduce_part(b):
         j, _ = second_hop
         part_push(j, b, part_a, pa_send, pa_sem, me).wait_recv()
-        acc[b, :, rows(j)] += part_a[b]
+        slot = lax.rem(b, RING) if not isinstance(b, int) else b % RING
+        ring[slot, :, rows(j)] += part_a[b]
 
     def send_reduced(b):
         j, to = second_hop
@@ -168,6 +163,12 @@
     def send_parts(b):
         for j, dst, send_sem, recv_sem, to in first_hop:
             part_push(j, b, dst, send_sem, recv_sem, to).start()
+
+    def sent(b):
+        for j, dst, send_sem, recv_sem, to in first_hop:
+            part_push(j, b, dst, send_sem, recv_sem, to).wait_send()
+        if second_hop is not None:
+            part_push(second_hop[0], b, part_b, red_send, pb_sem, second_hop[1]).wait_send()
 
     lag = 1 if me == 3 else 3
 
@@ -175,7 +176,8 @@
         cur, prev = lax.rem(b, 3), lax.rem(b + 2, 3)
         tcur, tprev = lax.rem(b, 2), lax.rem(b + 1, 2)
         b_prev = jnp.maximum(b - 1, 0)
-        acc_prev = jnp.where(b == 0, n_batch, b - 1)
+        own_prev = jnp.where(b == 0, n_batch, b - 1)
+        ring_cur, ring_prev = lax.rem(b, RING), lax.rem(b + RING - 1, RING)
 
         @pl.when(b + 1 < n_batch)
         def _():
@@ -183,10 +185,8 @@
             q_copy(b + 1, nxt).start()
             do_copy(b + 1, nxt).start()
 
-        @pl.when(b >= 3)
-        def _():
-            o_copy(b - 3, cur).wait()
-            dq_copy(b - 3, cur).wait()
+        if me > 0:
+            pl.when(b >= RING)(lambda: sent(b - RING))
 
         if relay is not None:
 
@@ -202,18 +202,13 @@
         kt[tcur, :, :width] = kv[0, b, :width].T
         vt[tcur, :, :width] = kv[1, b, :width].T
         for x in range(6):
-            here = (b, b, cur, tcur)
-            before = (b_prev, acc_prev, prev, tprev)
+            here = (b, b, ring_cur, cur, tcur)
+            before = (b_prev, own_prev, ring_prev, prev, tprev)
             sub_step(x, [here + (x - k,) if x >= k else before + (x - k + 6,) for k in range(5)])
         pl.when(b >= 1)(lambda: send_parts(b - 1))
         if second_hop is not None:
             pl.when(b >= lag)(lambda: reduce_part(b - lag))
 
-        @pl.when(b >= 1)
-        def _():
-            o_copy(b - 1, prev).start()
-            dq_copy(b - 1, prev).start()
-
         if second_hop is not None:
             pl.when(b >= lag)(lambda: send_reduced(b - lag))
         return carry
@@ -222,7 +217,7 @@
 
     last = n_batch - 1
     ls = last % 3
-    end = (last, last, ls, last % 2)
+    end = (last, last, last % RING, ls, last % 2)
     for x in range(3):
         sub_step(x, [end + (x - k + 6,) if k > x else None for k in range(5)])
     send_parts(last)
@@ -231,45 +226,34 @@
     sub_step(3, [None, None, None, None, end + (5,)])
     if me == 3:
         send_reduced(last)
-    o_copy(last, ls).start()
-    dq_copy(last, ls).start()
     if me == 2:
         for b in range(n_batch - lag, n_batch):
             reduce_part(b)
             send_reduced(b)
 
     def finalize(b, carry):
-        total = acc[b, :, own]
+        total = own_acc[b]
         if me == 0:
             part_push(0, b, part_a, pa_send, pa_sem, me).wait_recv()
             total = total + part_a[b]
         if me < 3:
             part_push(0, b, part_b, pb_send, pb_sem, me).wait_recv()
             total = total + part_b[b]
-        grads[b, 0] = (total[0] * scale).astype(BF16)
-        grads[b, 1] = total[1].astype(BF16)
-        pltpu.make_async_copy(grads.at[b, 0], dk_hbm.at[b], dk_sem.at[0]).start()
-        pltpu.make_async_copy(grads.at[b, 1], dv_hbm.at[b], dk_sem.at[1]).start()
+        dk_out[b] = (total[0] * scale).astype(BF16)
+        dv_out[b] = total[1].astype(BF16)
         return carry
 
     lax.fori_loop(0, n_batch, finalize, 0)
 
-    for b in range(n_batch - 3, n_batch):
-        o_copy(b, b % 3).wait()
-        dq_copy(b, b % 3).wait()
-    pltpu.make_async_copy(grads.at[:, 0], dk_hbm, dk_sem.at[0]).wait()
-    pltpu.make_async_copy(grads.at[:, 1], dv_hbm, dk_sem.at[1]).wait()
+    if me > 0:
+        for b in range(n_batch - RING, n_batch):
+            sent(b)
     for slot in range(len(direct)):
         for a, src in enumerate((k_hbm, v_hbm)):
             remote(src, kv.at[a, :, own], kv_send.at[2 * slot, a], kv_sem.at[a, 0, 0], me).wait_send()
     if relay is not None:
         for a in range(2):
             remote(kv.at[a, :, rows(relay[0])], kv.at[a, :, own], kv_send.at[1, a], kv_sem.at[a, 0, 0], me).wait_send()
-    every = pl.ds(0, n_batch)
-    for j, dst, send_sem, _, _ in first_hop:
-        remote(acc.at[every, :, rows(j)], dst, send_sem, pa_sem.at[0], me).wait_send()
-    if second_hop is not None:
-        remote(acc.at[every, :, rows(second_hop[0])], part_b, red_send, pa_sem.at[0], me).wait_send()
 
 
 def kernel(n_ctx, n_batch, scale, *refs):
@@ -280,6 +264,20 @@
     pl.semaphore_wait(barrier, n_ctx - 1)
     for i in range(n_ctx):
         pl.when(me == i)(functools.partial(device_program, i, n_batch, scale, refs))
+
+
+def put(*refs):
+    results, outs, sem = refs[:4], refs[4:8], refs[8]
+    copies = []
+    for i, (result, out) in enumerate(zip(results, outs)):
+        n = result.shape[0] // CHUNKS
+        for c in range(CHUNKS):
+            part = pl.ds(c * n, n)
+            copies.append(pltpu.make_async_copy(result.at[part], out.at[part], sem.at[i, c]))
+    for copy in copies:
+        copy.start()
+    for copy in copies:
+        copy.wait()
 
 
 def solution(mesh):
@@ -295,26 +293,34 @@
         vmem, dma = pltpu.VMEM, pltpu.SemaphoreType.DMA
         scratch = [
             vmem((2, n_batch, width, d_head), BF16),
-            vmem((n_batch + 1, 2, width, d_head), F32),
+            vmem((n_batch + 1, 2, c_len, d_head), F32),
+            vmem((RING, 2, width - c_len, d_head), F32),
             vmem((n_batch, 2, c_len, d_head), F32),
             vmem((n_batch, 2, c_len, d_head), F32),
-            vmem((n_batch, 2, c_len, d_head), BF16),
         ]
-        scratch += [vmem((3, n_q, c_len, d_head), BF16)] * 4
+        scratch += [vmem((3, n_q, c_len, d_head), BF16)] * 2
         scratch += [vmem((width, 256), F32)] * 7 + [vmem((width, 256), BF16)] * 5
         scratch += [vmem((2, 8, 256), F32), vmem((3, 8, 256), F32), vmem((2, 8, 256), F32)] + [vmem((2, d_head, width), BF16)] * 2
-        scratch += [dma((2,)), dma((2, n_ctx, n_batch)), dma((3, 2)), dma((n_batch,)), dma((n_batch,)), dma, dma, dma]
-        scratch += [dma((3,))] * 4 + [dma((2,))]
+        scratch += [dma((2,)), dma((2, n_ctx, n_batch)), dma((3, 2)), dma((n_batch,)), dma((n_batch,))] + [dma((RING,))] * 3
+        scratch += [dma((3,))] * 2
         hbm = pl.BlockSpec(memory_space=pl.ANY)
-        out_q, out_k = jax.ShapeDtypeStruct(q.shape, BF16), jax.ShapeDtypeStruct(k.shape, BF16)
+        local = pl.BlockSpec(memory_space=pltpu.VMEM)
+        results = pl.pallas_call(
+            functools.partial(kernel, n_ctx, n_batch, d_head ** -0.5),
+            out_shape=[pltpu.VMEM(x.shape, BF16) for x in (q, q, k, v)],
+            in_specs=[hbm] * 4,
+            out_specs=[local] * 4,
+            scratch_shapes=scratch,
+            compiler_params=pltpu.CompilerParams(collective_id=0, has_side_effects=True, vmem_limit_bytes=35 * 2 ** 20),
+        )(q, do, k, v)
         out, grad_q, grad_k, grad_v = pl.pallas_call(
-            functools.partial(kernel, n_ctx, n_batch, d_head ** -0.5),
-            out_shape=[out_q, out_q, out_k, out_k],
-            in_specs=[hbm] * 4,
+            put,
+            out_shape=[jax.ShapeDtypeStruct(x.shape, BF16) for x in (q, q, k, v)],
+            in_specs=[local] * 4,
             out_specs=[hbm] * 4,
-            scratch_shapes=scratch,
-            compiler_params=pltpu.CompilerParams(collective_id=0, has_side_effects=True, vmem_limit_bytes=62 * 2 ** 20),
-        )(q, do, k, v)
+            scratch_shapes=[dma((4, CHUNKS))],
+            compiler_params=pltpu.CompilerParams(vmem_limit_bytes=2 ** 20),
+        )(*results)
         return jnp.transpose(out, heads), jnp.transpose(grad_q, heads), grad_k.reshape(keys.shape), grad_v.reshape(values.shape)
 
     return jax.shard_map(local_step, mesh=mesh, in_specs=(part_spec,) * 4, out_specs=(part_spec,) * 4, check_vma=False)

time: 135 us -> 123 us (0.911)
  local copies, waits for them, and re-layouts: 19.5 us -> 0 us
  Pallas kernels: 114 us -> 122 us
    unnamed x10 -> x0, local copies, waits for them, and re-layouts: 19.5 us -> none
    pallas_call x0 -> x1, Pallas kernels: none -> 9.14 us  [local_step(): pl.pallas_call(put, out_shape=[jax.ShapeDtypeStruct(x.shape, BF16) for x...]
where the time goes in v3:
time: 123 us
  Pallas kernels  122 us (99%)
    pallas_call x1, Pallas kernels, local_step(): pl.pallas_call(functools.partial(kernel, n_ctx, n_batch, d_head ** (-0.5)...  113 us
    pallas_call x1, Pallas kernels, local_step(): pl.pallas_call(put, out_shape=[jax.ShapeDtypeStruct(x.shape, BF16) for x...  9.14 us

profile of v3, /device:TPU:0, one launch (start us, length us, event | category | flops | bytes accessed | tf_op | source)
XLA Modules:
  0.0 123.0 jit_solution(6140350783074764007)
XLA Ops:
  0.6 113.2 %shard_map.75 = (bf16[32,12,128,128]{3,2,1,0:T(8,128)(2,1)S(1)}, bf16[32,12,128,128]{3,2,1,0:T(8,128)(2,1)S(1)}, bf16[32,128,128]{2,1,0:T(8,128)(2,1)S(1)}, bf16[32,128,128]{2,1,0:T(8,128)(2,1)S(1)}) custom-call(bf16[32,12,128,128]{3,2,1,0:T(8,128)(2,1)} %bitcast.12, bf16[32,12,128,128]{3,2,1,0:T(8,128)(2,1)} %bitcast.13, bf16[32,128,128]{2,1,0:T(8,128)(2,1)} %bitcast.14, ...), custom_call_target="tpu_custom_call" | custom-call | tf_op jit(solution)/shard_map/pallas_call | solution.py:308
  113.8 9.1 %shard_map.76 = (bf16[32,12,128,128]{3,2,1,0:T(8,128)(2,1)}, bf16[32,12,128,128]{3,2,1,0:T(8,128)(2,1)}, bf16[32,128,128]{2,1,0:T(8,128)(2,1)}, bf16[32,128,128]{2,1,0:T(8,128)(2,1)}) custom-call(bf16[32,12,128,128]{3,2,1,0:T(8,128)(2,1)S(1)} %get-tuple-element.12.refs_0_, bf16[32,12,128,128]{3,2,1,0:T(8,128)(2,1)S(1)} %get-tuple-element.13.refs_1_, ...), custom_call_target="tpu_custom_call" | custom-call | tf_op jit(solution)/shard_map/pallas_call | solution.py:316

commit v4 on v3

--- a/solution.py
+++ b/solution.py
@@ -11,9 +11,10 @@
 LOG2E = 1.4426950408889634
 NEG_BIG = -1e30
 MESH = pl.DeviceIdType.MESH
-RELAY_AHEAD = 1
 RING = 8
 CHUNKS = 4
+FLIP_AT = 1
+TAIL = 3
 PIECE = 32
 
 
@@ -26,7 +27,7 @@
 
 
 def device_program(me, n_batch, scale, refs):
-    (q_hbm, do_hbm, k_hbm, v_hbm, o_out, dq_out, dk_out, dv_out,
+    (q_hbm, do_hbm, k_hbm, v_hbm, o_out, dq_out, dk_out, dv_out, tail_send, tail_own,
      kv, own_acc, ring, part_a, part_b, q_buf, do_buf,
      s_0, s_1, p_0, p_1, p_2, dp_0, dp_1, ph_0, ph_1, ds_0, ds_1, pb_buf, max_s, inv_s, delta_s, kt, vt,
      own_sem, kv_sem, kv_send, pa_sem, pb_sem, pa_send, pb_send, red_send,
@@ -69,6 +70,11 @@
         for a in range(2):
             kv_push(a, kv.at[a, b, rows(j)], j, b, to, 1).start()
 
+    def kv_others(b):
+        for j in range(me):
+            if relay is None or j != relay[0]:
+                kv_wait(j, b)
+
     q_copy(0, 0).start()
     do_copy(0, 0).start()
     own_copy(0, k_hbm).start()
@@ -86,8 +92,7 @@
     own_copy(0, k_hbm).wait()
     own_copy(1, v_hbm).wait()
     if relay is not None:
-        for b in range(RELAY_AHEAD):
-            relay_block(b)
+        relay_block(0)
 
     causal_r = lax.broadcasted_iota(jnp.int32, (128, 256), 0)
     causal_c = lax.broadcasted_iota(jnp.int32, (128, 256), 1) & 127
@@ -95,7 +100,7 @@
     def pair(ref, slot, x):
         return ref[slot, 2 * x:2 * x + 2].reshape(256, 128)
 
-    def sub_step(x, stages):
+    def sub_step(x, stages, ahead=None):
         par = [(x - k) % 2 for k in range(5)]
         tri = [(x - k) % 3 for k in range(5)]
         s0, s1, s2, s3, s4 = stages
@@ -145,6 +150,9 @@
                     sum8 = part if sum8 is None else sum8 + part
             if s2 is not None:
                 dp_buf[par[2]][r] = dot(kv[1, s2[0], r], dot2)
+            if ahead is not None:
+                kt[ahead[1], :, r] = kv[0, ahead[0], r].T
+                vt[ahead[1], :, r] = kv[1, ahead[0], r].T
         if s1 is not None:
             inv_s[tri[1], 0:1] = 1.0 / jnp.sum(sum8, axis=0, keepdims=True)
         if s0 is not None:
@@ -167,14 +175,14 @@
     def sent(b):
         for j, dst, send_sem, recv_sem, to in first_hop:
             part_push(j, b, dst, send_sem, recv_sem, to).wait_send()
-        if second_hop is not None:
+        if second_hop is not None and (not isinstance(b, int) or b < remote_rows):
             part_push(second_hop[0], b, part_b, red_send, pb_sem, second_hop[1]).wait_send()
 
     lag = 1 if me == 3 else 3
+    remote_rows = n_batch - TAIL
 
     def step(b, carry):
         cur, prev = lax.rem(b, 3), lax.rem(b + 2, 3)
-        tcur, tprev = lax.rem(b, 2), lax.rem(b + 1, 2)
         b_prev = jnp.maximum(b - 1, 0)
         own_prev = jnp.where(b == 0, n_batch, b - 1)
         ring_cur, ring_prev = lax.rem(b, RING), lax.rem(b + RING - 1, RING)
@@ -190,60 +198,63 @@
 
         if relay is not None:
 
-            @pl.when(b + RELAY_AHEAD < n_batch)
-            def _():
-                relay_block(b + RELAY_AHEAD)
-
-        for j in range(me):
-            if relay is None or j != relay[0]:
-                kv_wait(j, b)
+            pl.when(b + 1 < n_batch)(lambda: relay_block(b + 1))
+        kv_others(b)
         q_copy(b, cur).wait()
         do_copy(b, cur).wait()
-        kt[tcur, :, :width] = kv[0, b, :width].T
-        vt[tcur, :, :width] = kv[1, b, :width].T
         for x in range(6):
-            here = (b, b, ring_cur, cur, tcur)
-            before = (b_prev, own_prev, ring_prev, prev, tprev)
-            sub_step(x, [here + (x - k,) if x >= k else before + (x - k + 6,) for k in range(5)])
+            here = (b, b, ring_cur, cur, cur)
+            before = (b_prev, own_prev, ring_prev, prev, prev)
+            sub_step(x, [here + (x - k,) if x >= k else before + (x - k + 6,) for k in range(5)], (b, cur) if x == FLIP_AT else None)
         pl.when(b >= 1)(lambda: send_parts(b - 1))
         if second_hop is not None:
             pl.when(b >= lag)(lambda: reduce_part(b - lag))
 
         if second_hop is not None:
-            pl.when(b >= lag)(lambda: send_reduced(b - lag))
+            pl.when((b >= lag) & (b - lag < remote_rows))(lambda: send_reduced(b - lag))
         return carry
 
     lax.fori_loop(0, n_batch, step, 0)
 
     last = n_batch - 1
     ls = last % 3
-    end = (last, last, last % RING, ls, last % 2)
+    end = (last, last, last % RING, ls, ls)
     for x in range(3):
         sub_step(x, [end + (x - k + 6,) if k > x else None for k in range(5)])
     send_parts(last)
     if me == 3:
         reduce_part(last)
     sub_step(3, [None, None, None, None, end + (5,)])
-    if me == 3:
-        send_reduced(last)
     if me == 2:
         for b in range(n_batch - lag, n_batch):
             reduce_part(b)
-            send_reduced(b)
-
-    def finalize(b, carry):
+            if b < remote_rows:
+                send_reduced(b)
+
+    def local_sum(b):
         total = own_acc[b]
         if me == 0:
             part_push(0, b, part_a, pa_send, pa_sem, me).wait_recv()
             total = total + part_a[b]
-        if me < 3:
+        if me == 2:
+            part_push(0, b, part_b, pb_send, pb_sem, me).wait_recv()
+            total = total + part_b[b]
+        return total
+
+    def finalize(b, carry):
+        total = local_sum(b)
+        if me < 2:
             part_push(0, b, part_b, pb_send, pb_sem, me).wait_recv()
             total = total + part_b[b]
         dk_out[b] = (total[0] * scale).astype(BF16)
         dv_out[b] = total[1].astype(BF16)
         return carry
 
-    lax.fori_loop(0, n_batch, finalize, 0)
+    for t in range(TAIL):
+        b = remote_rows + t
+        tail_own[t] = local_sum(b)
+        tail_send[t] = jnp.zeros((2, 128, 128), F32) if second_hop is None else ring[b % RING, :, rows(second_hop[0])]
+    lax.fori_loop(0, remote_rows, finalize, 0)
 
     if me > 0:
         for b in range(n_batch - RING, n_batch):
@@ -267,7 +278,7 @@
 
 
 def put(*refs):
-    results, outs, sem = refs[:4], refs[4:8], refs[8]
+    results, outs, sem = refs[:2], refs[2:4], refs[4]
     copies = []
     for i, (result, out) in enumerate(zip(results, outs)):
         n = result.shape[0] // CHUNKS
@@ -277,6 +288,22 @@
     for copy in copies:
         copy.start()
     for copy in copies:
+        copy.wait()
+
+
+def put_last(scale, dk_main, dv_main, own, received, dk_hbm, dv_hbm, dk_tail, dv_tail, sem):
+    n = dk_main.shape[0] - TAIL
+    main, tail = pl.ds(0, n), pl.ds(n, TAIL)
+    copies = [pltpu.make_async_copy(dk_main.at[main], dk_hbm.at[main], sem.at[0]), pltpu.make_async_copy(dv_main.at[main], dv_hbm.at[main], sem.at[1])]
+    for copy in copies:
+        copy.start()
+    total = own[...] + received[...]
+    dk_tail[...] = (total[:, 0] * scale).astype(BF16)
+    dv_tail[...] = total[:, 1].astype(BF16)
+    last = [pltpu.make_async_copy(dk_tail, dk_hbm.at[tail], sem.at[2]), pltpu.make_async_copy(dv_tail, dv_hbm.at[tail], sem.at[3])]
+    for copy in last:
+        copy.start()
+    for copy in copies + last:
         copy.wait()
 
 
@@ -300,27 +327,39 @@
         ]
         scratch += [vmem((3, n_q, c_len, d_head), BF16)] * 2
         scratch += [vmem((width, 256), F32)] * 7 + [vmem((width, 256), BF16)] * 5
-        scratch += [vmem((2, 8, 256), F32), vmem((3, 8, 256), F32), vmem((2, 8, 256), F32)] + [vmem((2, d_head, width), BF16)] * 2
+        scratch += [vmem((2, 8, 256), F32), vmem((3, 8, 256), F32), vmem((2, 8, 256), F32)] + [vmem((3, d_head, width), BF16)] * 2
         scratch += [dma((2,)), dma((2, n_ctx, n_batch)), dma((3, 2)), dma((n_batch,)), dma((n_batch,))] + [dma((RING,))] * 3
         scratch += [dma((3,))] * 2
         hbm = pl.BlockSpec(memory_space=pl.ANY)
         local = pl.BlockSpec(memory_space=pltpu.VMEM)
-        results = pl.pallas_call(
-            functools.partial(kernel, n_ctx, n_batch, d_head ** -0.5),
-            out_shape=[pltpu.VMEM(x.shape, BF16) for x in (q, q, k, v)],
+        scale = d_head ** -0.5
+        tail = (TAIL, 2, c_len, d_head)
+        out, grad_q, grad_k, grad_v, tail_send, tail_own = pl.pallas_call(
+            functools.partial(kernel, n_ctx, n_batch, scale),
+            out_shape=[pltpu.VMEM(x.shape, BF16) for x in (q, q, k, v)] + [pltpu.VMEM(tail, F32), pltpu.VMEM(tail, F32)],
             in_specs=[hbm] * 4,
-            out_specs=[local] * 4,
+            out_specs=[local] * 6,
             scratch_shapes=scratch,
             compiler_params=pltpu.CompilerParams(collective_id=0, has_side_effects=True, vmem_limit_bytes=35 * 2 ** 20),
         )(q, do, k, v)
-        out, grad_q, grad_k, grad_v = pl.pallas_call(
+        received = lax.ppermute(tail_send, "ctx", [(2, 0), (3, 1)])
+        out, grad_q = pl.pallas_call(
             put,
-            out_shape=[jax.ShapeDtypeStruct(x.shape, BF16) for x in (q, q, k, v)],
+            out_shape=[jax.ShapeDtypeStruct(q.shape, BF16)] * 2,
+            in_specs=[local] * 2,
+            out_specs=[hbm] * 2,
+            scratch_shapes=[dma((2, CHUNKS))],
+            cost_estimate=pl.CostEstimate(flops=10 ** 10, bytes_accessed=2 * q.size * 2, transcendentals=0),
+            compiler_params=pltpu.CompilerParams(vmem_limit_bytes=2 ** 20),
+        )(out, grad_q)
+        grad_k, grad_v = pl.pallas_call(
+            functools.partial(put_last, scale),
+            out_shape=[jax.ShapeDtypeStruct(k.shape, BF16)] * 2,
             in_specs=[local] * 4,
-            out_specs=[hbm] * 4,
-            scratch_shapes=[dma((4, CHUNKS))],
-            compiler_params=pltpu.CompilerParams(vmem_limit_bytes=2 ** 20),
-        )(*results)
+            out_specs=[hbm] * 2,
+            scratch_shapes=[vmem((TAIL, c_len, d_head), BF16)] * 2 + [dma((4,))],
+            compiler_params=pltpu.CompilerParams(vmem_limit_bytes=4 * 2 ** 20),
+        )(grad_k, grad_v, tail_own, received)
         return jnp.transpose(out, heads), jnp.transpose(grad_q, heads), grad_k.reshape(keys.shape), grad_v.reshape(values.shape)
 
     return jax.shard_map(local_step, mesh=mesh, in_specs=(part_spec,) * 4, out_specs=(part_spec,) * 4, check_vma=False)

time: 123 us -> 119 us (0.967)
  Pallas kernels: 122 us -> 114 us
  waiting for transfers between devices: 0 us -> 2.33 us
  starting transfers between devices: 0 us -> 1.29 us
    pallas_call x2 -> x3, Pallas kernels: 122 us -> 114 us  [the longest x1 105 us: local_step(): pl.pallas_call(functools.partial(kernel, n_ctx, n_batch, scale), out_shap...]
    ppermute x0 -> x1, waiting for transfers between devices: none -> 2.33 us  [local_step(): received = lax.ppermute(tail_send, 'ctx', [(2, 0), (3, 1)])]
    ppermute x0 -> x1, starting transfers between devices: none -> 1.29 us  [local_step(): received = lax.ppermute(tail_send, 'ctx', [(2, 0), (3, 1)])]
  transfers between devices with their start and end apart: 0 -> 1, of which waited for: 0 -> 1; matrix products, arithmetic and copies ran while one was open for 0% -> 0% of each run, Pallas kernels for 0% -> 7%
where the time goes in v4:
time: 119 us
  Pallas kernels  114 us (96%)
  waiting for transfers between devices  2.33 us (2%)
  starting transfers between devices  1.29 us (1%)
    pallas_call x1, Pallas kernels, local_step(): pl.pallas_call(functools.partial(kernel, n_ctx, n_batch, scale), out_shap...  105 us
    pallas_call x1, Pallas kernels, local_step(): pl.pallas_call(put, out_shape=[jax.ShapeDtypeStruct(q.shape, BF16)] * 2,...  8.54 us
  transfers between devices with their start and end apart: 1, of which 1 were waited for; matrix products, arithmetic and copies ran while one was open for 0% of the time, Pallas kernels for 7%

profile of v4, /device:TPU:0, one launch (start us, length us, event | category | flops | bytes accessed | tf_op | source)
XLA Modules:
  0.0 118.7 jit_solution(12494571498707265216)
XLA Ops:
  0.6 104.6 %shard_map.75 = (bf16[32,12,128,128]{3,2,1,0:T(8,128)(2,1)S(1)}, bf16[32,12,128,128]{3,2,1,0:T(8,128)(2,1)S(1)}, bf16[32,128,128]{2,1,0:T(8,128)(2,1)S(1)}, bf16...) custom-call(bf16[32,12,128,128]{3,2,1,0:T(8,128)(2,1)} %bitcast.12, ...), custom_call_target="tpu_custom_call" | custom-call | tf_op jit(solution)/shard_map/pallas_call | solution.py:337
  105.2 1.3 %collective-permute-start = (f32[3,2,128,128]{3,2,1,0:T(8,128)S(1)}, f32[3,2,128,128]{3,2,1,0:T(8,128)S(1)}, u32[]{:S(2)}, u32[]{:S(2)}) collective-permute-start(f32[3,2,128,128]{3,2,1,0:T(8,128)S(1)} %get-tuple-element.21), channel_id=1, source_target_pairs={{2,0},{3,1},{6,4},{7,5}} | collective-permute-start | bytes 1179656 | tf_op jit(solution)/shard_map/ppermute | solution.py:345
  106.5 8.5 %shard_map.76 = (bf16[32,12,128,128]{3,2,1,0:T(8,128)(2,1)}, bf16[32,12,128,128]{3,2,1,0:T(8,128)(2,1)}) custom-call(bf16[32,12,128,128]{3,2,1,0:T(8,128)(2,1)S(1)} %get-tuple-element.14.refs_0_, bf16[32,12,128,128]{3,2,1,0:T(8,128)(2,1)S(1)} %get-tuple-element.15.refs_1_), custom_call_target="tpu_custom_call" | custom-call | flops 10000000000 | bytes 25165824 | tf_op jit(solution)/shard_map/pallas_call | solution.py:346
  115.1 2.3 %collective-permute-done.received = f32[3,2,128,128]{3,2,1,0:T(8,128)S(1)} collective-permute-done((f32[3,2,128,128]{3,2,1,0:T(8,128)S(1)}, f32[3,2,128,128]{3,2,1,0:T(8,128)S(1)}, u32[]{:S(2)}, u32[]{:S(2)}) %collective-permute-start) | collective-permute-done | bytes 393248 | tf_op jit(solution)/shard_map/ppermute | solution.py:345
  117.4 1.3 %shard_map.77 = (bf16[32,128,128]{2,1,0:T(8,128)(2,1)}, bf16[32,128,128]{2,1,0:T(8,128)(2,1)}) custom-call(bf16[32,128,128]{2,1,0:T(8,128)(2,1)S(1)} %get-tuple-element.18.dk_main, bf16[32,128,128]{2,1,0:T(8,128)(2,1)S(1)} %get-tuple-element.19.dv_main, f32[3,2,128,128]{3,2,1,0:T(8,128)S(1)} %get-tuple-element.20.own, ...), custom_call_target="tpu_custom_call" | custom-call | tf_op jit(solution)/shard_map/pallas_call | solution.py:355
Async XLA Ops:
  105.2 12.2 %collective-permute-start = (f32[3,2,128,128]{3,2,1,0:T(8,128)S(1)}, f32[3,2,128,128]{3,2,1,0:T(8,128)S(1)}, u32[]{:S(2)}, u32[]{:S(2)}) collective-permute-start(f32[3,2,128,128]{3,2,1,0:T(8,128)S(1)} %get-tuple-element.21), channel_id=1, source_target_pairs={{2,0},{3,1},{6,4},{7,5}} | collective-permute-start | bytes 1179656 | tf_op jit(solution)/shard_map/ppermute | solution.py:345

commit v5 on v4

--- a/solution.py
+++ b/solution.py
@@ -14,7 +14,7 @@
 RING = 8
 CHUNKS = 4
 FLIP_AT = 1
-TAIL = 3
+TAIL = 2
 PIECE = 32
 
 
@@ -75,20 +75,21 @@
             if relay is None or j != relay[0]:
                 kv_wait(j, b)
 
+    direct = {0: (2, 1), 1: (3,), 2: (3,), 3: ()}[me]
+
+    def push_own(b, carry):
+        for slot, to in enumerate(direct):
+            for a, src in enumerate((k_hbm, v_hbm)):
+                kv_push(a, src.at[b], me, b, to, 2 * slot).start()
+        return carry
+
+    push_own(0, 0)
+    own_copy(0, k_hbm).start()
+    own_copy(1, v_hbm).start()
     q_copy(0, 0).start()
     do_copy(0, 0).start()
-    own_copy(0, k_hbm).start()
-    own_copy(1, v_hbm).start()
-    direct = {0: (2, 1), 1: (3,), 2: (3,), 3: ()}[me]
     if direct:
-
-        def push_own(b, carry):
-            for slot, to in enumerate(direct):
-                for a, src in enumerate((k_hbm, v_hbm)):
-                    kv_push(a, src.at[b], me, b, to, 2 * slot).start()
-            return carry
-
-        lax.fori_loop(0, n_batch, push_own, 0)
+        lax.fori_loop(1, n_batch, push_own, 0)
     own_copy(0, k_hbm).wait()
     own_copy(1, v_hbm).wait()
     if relay is not None:
@@ -178,7 +179,7 @@
         if second_hop is not None and (not isinstance(b, int) or b < remote_rows):
             part_push(second_hop[0], b, part_b, red_send, pb_sem, second_hop[1]).wait_send()
 
-    lag = 1 if me == 3 else 3
+    lag = 1 if me == 3 else 2
     remote_rows = n_batch - TAIL
 
     def step(b, carry):

time: 119 us -> 118 us (level)
  waiting for transfers between devices: 2.33 us -> 0.01 us
    ppermute x1, waiting for transfers between devices: 2.33 us -> 0.01 us  [local_step(): received = lax.ppermute(tail_send, 'ctx', [(2, 0), (3, 1)])]
  transfers between devices with their start and end apart: 1 -> 1, of which waited for: 1 -> 0; matrix products, arithmetic and copies ran while one was open for 0% -> 0% of each run, Pallas kernels for 7% -> 7%
where the time goes in v5:
time: 118 us; the launch traced here: 117 us
  Pallas kernels  115 us (97%)
  starting transfers between devices  1.29 us (1%)
    pallas_call x1, Pallas kernels, local_step(): pl.pallas_call(functools.partial(kernel, n_ctx, n_batch, scale), out_shap...  105 us
    pallas_call x1, Pallas kernels, local_step(): pl.pallas_call(put, out_shape=[jax.ShapeDtypeStruct(q.shape, BF16)] * 2,...  8.54 us
  transfers between devices with their start and end apart: 1, of which 0 were waited for; matrix products, arithmetic and copies ran while one was open for 0% of the time, Pallas kernels for 7%

profile of v5, /device:TPU:0, one launch (start us, length us, event | category | flops | bytes accessed | tf_op | source)
XLA Modules:
  0.0 116.9 jit_solution(4564685374038455883)
XLA Ops:
  0.6 105.0 %shard_map.75 = (bf16[32,12,128,128]{3,2,1,0:T(8,128)(2,1)S(1)}, bf16[32,12,128,128]{3,2,1,0:T(8,128)(2,1)S(1)}, bf16[32,128,128]{2,1,0:T(8,128)(2,1)S(1)}, bf16...) custom-call(bf16[32,12,128,128]{3,2,1,0:T(8,128)(2,1)} %bitcast.12, ...), custom_call_target="tpu_custom_call" | custom-call | tf_op jit(solution)/shard_map/pallas_call | solution.py:338
  105.7 1.3 %collective-permute-start = (f32[2,2,128,128]{3,2,1,0:T(8,128)S(1)}, f32[2,2,128,128]{3,2,1,0:T(8,128)S(1)}, u32[]{:S(2)}, u32[]{:S(2)}) collective-permute-start(f32[2,2,128,128]{3,2,1,0:T(8,128)S(1)} %get-tuple-element.21), channel_id=1, source_target_pairs={{2,0},{3,1},{6,4},{7,5}} | collective-permute-start | bytes 786440 | tf_op jit(solution)/shard_map/ppermute | solution.py:346
  107.0 8.5 %shard_map.76 = (bf16[32,12,128,128]{3,2,1,0:T(8,128)(2,1)}, bf16[32,12,128,128]{3,2,1,0:T(8,128)(2,1)}) custom-call(bf16[32,12,128,128]{3,2,1,0:T(8,128)(2,1)S(1)} %get-tuple-element.14.refs_0_, bf16[32,12,128,128]{3,2,1,0:T(8,128)(2,1)S(1)} %get-tuple-element.15.refs_1_), custom_call_target="tpu_custom_call" | custom-call | flops 10000000000 | bytes 25165824 | tf_op jit(solution)/shard_map/pallas_call | solution.py:347
  115.5 0.0 collective-permute-done.received
  115.5 1.3 %shard_map.77 = (bf16[32,128,128]{2,1,0:T(8,128)(2,1)}, bf16[32,128,128]{2,1,0:T(8,128)(2,1)}) custom-call(bf16[32,128,128]{2,1,0:T(8,128)(2,1)S(1)} %get-tuple-element.18.dk_main, bf16[32,128,128]{2,1,0:T(8,128)(2,1)S(1)} %get-tuple-element.19.dv_main, f32[2,2,128,128]{3,2,1,0:T(8,128)S(1)} %get-tuple-element.20.own, ...), custom_call_target="tpu_custom_call" | custom-call | tf_op jit(solution)/shard_map/pallas_call | solution.py:356
Async XLA Ops:
  105.7 9.8 %collective-permute-start = (f32[2,2,128,128]{3,2,1,0:T(8,128)S(1)}, f32[2,2,128,128]{3,2,1,0:T(8,128)S(1)}, u32[]{:S(2)}, u32[]{:S(2)}) collective-permute-start(f32[2,2,128,128]{3,2,1,0:T(8,128)S(1)} %get-tuple-element.21), channel_id=1, source_target_pairs={{2,0},{3,1},{6,4},{7,5}} | collective-permute-start | bytes 786440 | tf_op jit(solution)/shard_map/ppermute | solution.py:346

commit v6 on v5

--- a/solution.py
+++ b/solution.py
@@ -11,10 +11,10 @@
 LOG2E = 1.4426950408889634
 NEG_BIG = -1e30
 MESH = pl.DeviceIdType.MESH
-RING = 8
+RING = 9
 CHUNKS = 4
 FLIP_AT = 1
-TAIL = 2
+TAIL = 3
 PIECE = 32
 
 
@@ -31,9 +31,10 @@
      kv, own_acc, ring, part_a, part_b, q_buf, do_buf,
      s_0, s_1, p_0, p_1, p_2, dp_0, dp_1, ph_0, ph_1, ds_0, ds_1, pb_buf, max_s, inv_s, delta_s, kt, vt,
      own_sem, kv_sem, kv_send, pa_sem, pb_sem, pa_send, pb_send, red_send,
-     q_sem, do_sem) = refs
+     q_sem, do_sem, x_q, x_do, x_acc, x_sem, x_send, xo_sem, xo_send, xa_send) = refs
     blocks = me + 1
-    width = blocks * 128
+    remote_rows = n_batch - TAIL
+    n_rows = remote_rows if me == 3 else n_batch
     s_buf, p_buf, dp_buf, ph_buf, ds_buf = (s_0, s_1), (p_0, p_1, p_2), (dp_0, dp_1), (ph_0, ph_1), (ds_0, ds_1)
     own = pl.ds(me * 128, 128)
 
@@ -74,6 +75,20 @@
         for j in range(me):
             if relay is None or j != relay[0]:
                 kv_wait(j, b)
+
+    def extra_in(e, to):
+        b = remote_rows + e
+        moves = [remote(q_hbm.at[b], x_q.at[e], x_send.at[0, e], x_sem.at[0, e], to), remote(do_hbm.at[b], x_do.at[e], x_send.at[1, e], x_sem.at[1, e], to)]
+        for a, src in enumerate((k_hbm, v_hbm)):
+            moves.append(remote(src.at[b], kv.at[a, b, rows(3)], x_send.at[2 + a, e], kv_sem.at[a, 3, b], to))
+        return moves
+
+    def extra_out(e, to):
+        b = remote_rows + e
+        return [remote(q_buf.at[e], o_out.at[b], xo_send.at[0, e], xo_sem.at[0, e], to), remote(do_buf.at[e], dq_out.at[b], xo_send.at[1, e], xo_sem.at[1, e], to)]
+
+    def extra_acc(e, to):
+        return remote(x_acc.at[e], part_b.at[remote_rows + e], xa_send.at[e], pb_sem.at[remote_rows + e], to)
 
     direct = {0: (2, 1), 1: (3,), 2: (3,), 3: ()}[me]
 
@@ -101,18 +116,31 @@
     def pair(ref, slot, x):
         return ref[slot, 2 * x:2 * x + 2].reshape(256, 128)
 
-    def sub_step(x, stages, ahead=None):
+    def main_acc(j, s3):
+        return (own_acc, (s3[1],), True) if j == me else (ring, (s3[2],), True)
+
+    def extra_row_acc(j, s3):
+        if j == 3:
+            return x_acc, (s3[1] - remote_rows,), True
+        return (own_acc, (s3[1],), False) if j == me else (ring, (s3[2],), False)
+
+    main_cfg = (blocks, q_buf, do_buf, o_out, dq_out, 0, main_acc)
+    extra_cfg = (blocks + 1, x_q, x_do, q_buf, do_buf, 3, extra_row_acc)
+
+    def sub_step(x, stages, ahead=None, cfg=main_cfg):
+        blocks, q_src, do_src, o_dst, dq_dst, at, acc_of = cfg
+        width = blocks * 128
         par = [(x - k) % 2 for k in range(5)]
         tri = [(x - k) % 3 for k in range(5)]
         s0, s1, s2, s3, s4 = stages
         if s0 is not None:
-            qt0 = pair(q_buf, s0[3], s0[5]).T
+            qt0 = pair(q_src, s0[3], s0[5]).T
         if s2 is not None:
-            dot2 = pair(do_buf, s2[3], s2[5]).T
+            dot2 = pair(do_src, s2[3], s2[5]).T
         if s1 is not None:
             max1 = max_s[par[1], 0:1]
         if s3 is not None:
-            q3, do3 = pair(q_buf, s3[3], s3[5]), pair(do_buf, s3[3], s3[5])
+            q3, do3 = pair(q_src, s3[3], s3[5]), pair(do_src, s3[3], s3[5])
             inv3, delta3 = inv_s[tri[3], 0:1], delta_s[par[3], 0:1]
         max8 = sum8 = None
         for j in range(blocks):
@@ -120,11 +148,11 @@
             pieces = [slice(y, y + PIECE) for y in range(j * 128, j * 128 + 128, PIECE)]
             if j == 0 and s2 is not None:
                 ot = (dot(vt[s2[4], :, :width], ph_buf[par[2]][:width]) * inv_s[tri[2], 0:1]).astype(BF16)
-                o_out[s2[0], 2 * s2[5]:2 * s2[5] + 2] = ot.T.reshape(2, 128, 128)
+                o_dst[s2[at], 2 * s2[5]:2 * s2[5] + 2] = ot.T.reshape(2, 128, 128)
                 delta_s[par[2], 0:1] = jnp.sum(dot2.astype(F32) * ot.astype(F32), axis=0, keepdims=True)
             if j == min(1, blocks - 1) and s4 is not None:
                 dq = (dot(kt[s4[4], :, :width], ds_buf[par[4]][:width]) * scale).astype(BF16)
-                dq_out[s4[0], 2 * s4[5]:2 * s4[5] + 2] = dq.T.reshape(2, 128, 128)
+                dq_dst[s4[at], 2 * s4[5]:2 * s4[5] + 2] = dq.T.reshape(2, 128, 128)
             if s3 is not None:
                 for y in pieces:
                     pb = p_buf[tri[3]][y] * inv3
@@ -132,9 +160,10 @@
                     pb_buf[y] = pb.astype(BF16)
                 dv = dot(pb_buf[r], do3)
                 dk = dot(ds_buf[par[3]][r], q3)
+                dst, idx, fresh = acc_of(j, s3)
                 for w, part in enumerate((dk, dv)):
-                    dst, at = (own_acc, (s3[1], w)) if j == me else (ring, (s3[2], w, r))
-                    dst[at] = part if s3[5] == 0 else dst[at] + part
+                    where = idx + ((w,) if dst is not ring else (w, r))
+                    dst[where] = part if fresh and s3[5] == 0 else dst[where] + part
             if s0 is not None:
                 st = dot(kv[0, s0[0], r], qt0)
                 if j == blocks - 1:
@@ -179,8 +208,9 @@
         if second_hop is not None and (not isinstance(b, int) or b < remote_rows):
             part_push(second_hop[0], b, part_b, red_send, pb_sem, second_hop[1]).wait_send()
 
-    lag = 1 if me == 3 else 2
-    remote_rows = n_batch - TAIL
+    def paced(b):
+        return jnp.maximum(b, 0) if me == 3 else jnp.maximum((82 * (b + 1) - 142) // 100, 0)
+
 
     def step(b, carry):
         cur, prev = lax.rem(b, 3), lax.rem(b + 2, 3)
@@ -188,7 +218,7 @@
         own_prev = jnp.where(b == 0, n_batch, b - 1)
         ring_cur, ring_prev = lax.rem(b, RING), lax.rem(b + RING - 1, RING)
 
-        @pl.when(b + 1 < n_batch)
+        @pl.when(b + 1 < n_rows)
         def _():
             nxt = lax.rem(b + 1, 3)
             q_copy(b + 1, nxt).start()
@@ -199,7 +229,11 @@
 
         if relay is not None:
 
-            pl.when(b + 1 < n_batch)(lambda: relay_block(b + 1))
+            if me == 2:
+                pl.when(b + 1 < n_batch)(lambda: relay_block(b + 1))
+            else:
+                pl.when((b >= 1) & (2 * b < n_batch))(lambda: relay_block(2 * b))
+                pl.when(2 * b + 1 < n_batch)(lambda: relay_block(2 * b + 1))
         kv_others(b)
         q_copy(b, cur).wait()
         do_copy(b, cur).wait()
@@ -207,37 +241,88 @@
             here = (b, b, ring_cur, cur, cur)
             before = (b_prev, own_prev, ring_prev, prev, prev)
             sub_step(x, [here + (x - k,) if x >= k else before + (x - k + 6,) for k in range(5)], (b, cur) if x == FLIP_AT else None)
-        pl.when(b >= 1)(lambda: send_parts(b - 1))
+        pl.when((b >= 1) & (b <= remote_rows) if me == 2 else b >= 1)(lambda: send_parts(b - 1))
+
         if second_hop is not None:
-            pl.when(b >= lag)(lambda: reduce_part(b - lag))
-
-        if second_hop is not None:
-            pl.when((b >= lag) & (b - lag < remote_rows))(lambda: send_reduced(b - lag))
+
+            @pl.when(paced(b) > paced(b - 1))
+            def _():
+                reduce_part(paced(b) - 1)
+                send_reduced(paced(b) - 1)
+
+        if me == 3:
+
+            @pl.when(b < TAIL)
+            def _():
+                for move in extra_in(b, 2):
+                    move.start()
+
         return carry
 
-    lax.fori_loop(0, n_batch, step, 0)
-
-    last = n_batch - 1
+    lax.fori_loop(0, n_rows, step, 0)
+
+    last = n_rows - 1
     ls = last % 3
     end = (last, last, last % RING, ls, ls)
     for x in range(3):
         sub_step(x, [end + (x - k + 6,) if k > x else None for k in range(5)])
-    send_parts(last)
+    if me != 2:
+        send_parts(last)
     if me == 3:
         reduce_part(last)
     sub_step(3, [None, None, None, None, end + (5,)])
+    if me == 3:
+        send_reduced(last)
+
+    def reduce_and_send(b):
+        reduce_part(b)
+        send_reduced(b)
+
     if me == 2:
-        for b in range(n_batch - lag, n_batch):
-            reduce_part(b)
-            if b < remote_rows:
-                send_reduced(b)
+        for b in range((82 * n_batch - 142) // 100, remote_rows - 1 - TAIL):
+            reduce_and_send(b)
+
+        def extra(e, carry):
+            b = remote_rows + e
+            prev = lax.rem(e + 2, 3)
+            here = (b, b, lax.rem(b, RING), e, e)
+            before = (jnp.maximum(b - 1, remote_rows), jnp.where(e == 0, n_batch, b - 1), jnp.where(e == 0, RING, lax.rem(b - 1, RING)), prev, prev)
+            for x in range(6):
+                sub_step(x, [here + (x - k,) if x >= k else before + (x - k + 6,) for k in range(5)], (b, e) if x == FLIP_AT else None, extra_cfg)
+
+            @pl.when(e >= 1)
+            def _():
+                for move in extra_out(e - 1, 3):
+                    move.start()
+                extra_acc(e - 1, 3).start()
+                send_parts(b - 1)
+
+            reduce_and_send(remote_rows - 1 - TAIL + e)
+            return carry
+
+        for e in range(TAIL):
+            for move in extra_in(e, me):
+                move.wait_recv()
+        lax.fori_loop(0, TAIL, extra, 0)
+        end = (n_batch - 1, n_batch - 1, (n_batch - 1) % RING, TAIL - 1, TAIL - 1)
+        for x in range(3):
+            sub_step(x, [end + (x - k + 6,) if k > x else None for k in range(5)], None, extra_cfg)
+        extra_acc(TAIL - 1, 3).start()
+        send_parts(n_batch - 1)
+        sub_step(3, [None, None, None, None, end + (5,)], None, extra_cfg)
+        reduce_and_send(remote_rows - 1)
+        for move in extra_out(TAIL - 1, 3):
+            move.start()
 
     def local_sum(b):
+        if me == 3 and isinstance(b, int) and b >= remote_rows:
+            extra_acc(b - remote_rows, me).wait_recv()
+            return part_b[b]
         total = own_acc[b]
         if me == 0:
             part_push(0, b, part_a, pa_send, pa_sem, me).wait_recv()
             total = total + part_a[b]
-        if me == 2:
+        if me == 2 and not (isinstance(b, int) and b >= remote_rows):
             part_push(0, b, part_b, pb_send, pb_sem, me).wait_recv()
             total = total + part_b[b]
         return total
@@ -254,12 +339,27 @@
     for t in range(TAIL):
         b = remote_rows + t
         tail_own[t] = local_sum(b)
-        tail_send[t] = jnp.zeros((2, 128, 128), F32) if second_hop is None else ring[b % RING, :, rows(second_hop[0])]
+        if me == 3:
+            part_push(1, b, part_a, pa_send, pa_sem, me).wait_recv()
+            tail_send[t] = part_a[b]
+        else:
+            tail_send[t] = jnp.zeros((2, 128, 128), F32) if second_hop is None else ring[b % RING, :, rows(second_hop[0])]
     lax.fori_loop(0, remote_rows, finalize, 0)
 
     if me > 0:
-        for b in range(n_batch - RING, n_batch):
+        for b in range(n_rows - RING, n_rows):
             sent(b)
+    if me == 2:
+        for e in range(TAIL):
+            for move in extra_out(e, 3) + [extra_acc(e, 3)]:
+                move.wait_send()
+    if me == 3:
+        for e in range(TAIL):
+            kv_others(remote_rows + e)
+            for move in extra_in(e, 2):
+                move.wait_send()
+            for move in extra_out(e, me):
+                move.wait_recv()
     for slot in range(len(direct)):
         for a, src in enumerate((k_hbm, v_hbm)):
             remote(src, kv.at[a, :, own], kv_send.at[2 * slot, a], kv_sem.at[a, 0, 0], me).wait_send()
@@ -322,7 +422,7 @@
         scratch = [
             vmem((2, n_batch, width, d_head), BF16),
             vmem((n_batch + 1, 2, c_len, d_head), F32),
-            vmem((RING, 2, width - c_len, d_head), F32),
+            vmem((RING + 1, 2, width - c_len, d_head), F32),
             vmem((n_batch, 2, c_len, d_head), F32),
             vmem((n_batch, 2, c_len, d_head), F32),
         ]
@@ -331,6 +431,8 @@
         scratch += [vmem((2, 8, 256), F32), vmem((3, 8, 256), F32), vmem((2, 8, 256), F32)] + [vmem((3, d_head, width), BF16)] * 2
         scratch += [dma((2,)), dma((2, n_ctx, n_batch)), dma((3, 2)), dma((n_batch,)), dma((n_batch,))] + [dma((RING,))] * 3
         scratch += [dma((3,))] * 2
+        scratch += [vmem((TAIL, n_q, c_len, d_head), BF16)] * 2 + [vmem((TAIL + 1, 2, c_len, d_head), F32)]
+        scratch += [dma((2, TAIL)), dma((4, TAIL)), dma((2, TAIL)), dma((2, TAIL)), dma((TAIL,))]
         hbm = pl.BlockSpec(memory_space=pl.ANY)
         local = pl.BlockSpec(memory_space=pltpu.VMEM)
         scale = d_head ** -0.5
@@ -341,7 +443,7 @@
             in_specs=[hbm] * 4,
             out_specs=[local] * 6,
             scratch_shapes=scratch,
-            compiler_params=pltpu.CompilerParams(collective_id=0, has_side_effects=True, vmem_limit_bytes=35 * 2 ** 20),
+            compiler_params=pltpu.CompilerParams(collective_id=0, has_side_effects=True, vmem_limit_bytes=37 * 2 ** 20),
         )(q, do, k, v)
         received = lax.ppermute(tail_send, "ctx", [(2, 0), (3, 1)])
         out, grad_q = pl.pallas_call(

time: 118 us -> 118 us (level)
  transfers between devices with their start and end apart: 1 -> 1, of which waited for: 0 -> 1; matrix products, arithmetic and copies ran while one was open for 0% -> 0% of each run, Pallas kernels for 7% -> 7%
where the time goes in v6:
time: 118 us
  Pallas kernels  115 us (97%)
  starting transfers between devices  1.28 us (1%)
    pallas_call x1, Pallas kernels, local_step(): pl.pallas_call(functools.partial(kernel, n_ctx, n_batch, scale), out_shap...  105 us
    pallas_call x1, Pallas kernels, local_step(): pl.pallas_call(put, out_shape=[jax.ShapeDtypeStruct(q.shape, BF16)] * 2,...  8.54 us
  transfers between devices with their start and end apart: 1, of which 1 were waited for; matrix products, arithmetic and copies ran while one was open for 0% of the time, Pallas kernels for 7%

profile of v6, /device:TPU:0, one launch (start us, length us, event | category | flops | bytes accessed | tf_op | source)
XLA Modules:
  0.0 117.8 jit_solution(14084042337284424804)
XLA Ops:
  0.6 104.8 %shard_map.75 = (bf16[32,12,128,128]{3,2,1,0:T(8,128)(2,1)S(1)}, bf16[32,12,128,128]{3,2,1,0:T(8,128)(2,1)S(1)}, bf16[32,128,128]{2,1,0:T(8,128)(2,1)S(1)}, bf16...) custom-call(bf16[32,12,128,128]{3,2,1,0:T(8,128)(2,1)} %bitcast.12, ...), custom_call_target="tpu_custom_call" | custom-call | tf_op jit(solution)/shard_map/pallas_call | solution.py:440
  105.4 0.0 copy-start
  105.5 0.7 copy-done
  106.2 1.3 %collective-permute-start = (f32[3,2,128,128]{3,2,1,0:T(8,128)}, f32[3,2,128,128]{3,2,1,0:T(8,128)S(1)}, u32[]{:S(2)}, u32[]{:S(2)}) collective-permute-start(f32[3,2,128,128]{3,2,1,0:T(8,128)} %copy-done), channel_id=1, source_target_pairs={{2,0},{3,1},{6,4},{7,5}} | collective-permute-start | bytes 1179656 | tf_op jit(solution)/shard_map/ppermute | solution.py:448
  107.5 8.5 %shard_map.76 = (bf16[32,12,128,128]{3,2,1,0:T(8,128)(2,1)}, bf16[32,12,128,128]{3,2,1,0:T(8,128)(2,1)}) custom-call(bf16[32,12,128,128]{3,2,1,0:T(8,128)(2,1)S(1)} %get-tuple-element.14.refs_0_, bf16[32,12,128,128]{3,2,1,0:T(8,128)(2,1)S(1)} %get-tuple-element.15.refs_1_), custom_call_target="tpu_custom_call" | custom-call | flops 10000000000 | bytes 25165824 | tf_op jit(solution)/shard_map/pallas_call | solution.py:449
  116.0 0.3 collective-permute-done.received
  116.3 1.3 %shard_map.77 = (bf16[32,128,128]{2,1,0:T(8,128)(2,1)}, bf16[32,128,128]{2,1,0:T(8,128)(2,1)}) custom-call(bf16[32,128,128]{2,1,0:T(8,128)(2,1)S(1)} %get-tuple-element.18.dk_main, bf16[32,128,128]{2,1,0:T(8,128)(2,1)S(1)} %get-tuple-element.19.dv_main, f32[3,2,128,128]{3,2,1,0:T(8,128)S(1)} %get-tuple-element.20.own, ...), custom_call_target="tpu_custom_call" | custom-call | tf_op jit(solution)/shard_map/pallas_call | solution.py:458
Async XLA Ops:
  105.4 0.7 copy-start
  106.2 10.1 %collective-permute-start = (f32[3,2,128,128]{3,2,1,0:T(8,128)}, f32[3,2,128,128]{3,2,1,0:T(8,128)S(1)}, u32[]{:S(2)}, u32[]{:S(2)}) collective-permute-start(f32[3,2,128,128]{3,2,1,0:T(8,128)} %copy-done), channel_id=1, source_target_pairs={{2,0},{3,1},{6,4},{7,5}} | collective-permute-start | bytes 1179656 | tf_op jit(solution)/shard_map/ppermute | solution.py:448

commit v7 on v6

--- a/solution.py
+++ b/solution.py
@@ -14,7 +14,7 @@
 RING = 9
 CHUNKS = 4
 FLIP_AT = 1
-TAIL = 3
+TAIL = 2
 PIECE = 32
 
 
@@ -279,12 +279,12 @@
         send_reduced(b)
 
     if me == 2:
-        for b in range((82 * n_batch - 142) // 100, remote_rows - 1 - TAIL):
+        for b in range((82 * n_batch - 142) // 100, remote_rows - 1 - 2 * TAIL):
             reduce_and_send(b)
 
         def extra(e, carry):
             b = remote_rows + e
-            prev = lax.rem(e + 2, 3)
+            prev = lax.rem(e + TAIL - 1, TAIL)
             here = (b, b, lax.rem(b, RING), e, e)
             before = (jnp.maximum(b - 1, remote_rows), jnp.where(e == 0, n_batch, b - 1), jnp.where(e == 0, RING, lax.rem(b - 1, RING)), prev, prev)
             for x in range(6):
@@ -297,7 +297,8 @@
                 extra_acc(e - 1, 3).start()
                 send_parts(b - 1)
 
-            reduce_and_send(remote_rows - 1 - TAIL + e)
+            reduce_and_send(remote_rows - 1 - 2 * TAIL + 2 * e)
+            reduce_and_send(remote_rows - 2 * TAIL + 2 * e)
             return carry
 
         for e in range(TAIL):

time: 118 us -> 120 us (1.017)
  Pallas kernels: 115 us -> 117 us
    pallas_call x1, Pallas kernels: 105 us -> 107 us  [local_step(): pl.pallas_call(functools.partial(kernel, n_ctx, n_batch, scale), out_shap...]
  transfers between devices with their start and end apart: 1 -> 1, of which waited for: 1 -> 0; matrix products, arithmetic and copies ran while one was open for 0% -> 0% of each run, Pallas kernels for 7% -> 7%
where the time goes in v7:
time: 120 us; the launch traced here: 119 us
  Pallas kernels  117 us (98%)
  starting transfers between devices  1.29 us (1%)
    pallas_call x1, Pallas kernels, local_step(): pl.pallas_call(functools.partial(kernel, n_ctx, n_batch, scale), out_shap...  107 us
    pallas_call x1, Pallas kernels, local_step(): pl.pallas_call(put, out_shape=[jax.ShapeDtypeStruct(q.shape, BF16)] * 2,...  8.54 us
  transfers between devices with their start and end apart: 1, of which 0 were waited for; matrix products, arithmetic and copies ran while one was open for 0% of the time, Pallas kernels for 7%

profile of v7, /device:TPU:0, one launch (start us, length us, event | category | flops | bytes accessed | tf_op | source)
XLA Modules:
  0.0 119.2 jit_solution(5753126975251445029)
XLA Ops:
  0.6 107.2 %shard_map.75 = (bf16[32,12,128,128]{3,2,1,0:T(8,128)(2,1)S(1)}, bf16[32,12,128,128]{3,2,1,0:T(8,128)(2,1)S(1)}, bf16[32,128,128]{2,1,0:T(8,128)(2,1)S(1)}, bf16...) custom-call(bf16[32,12,128,128]{3,2,1,0:T(8,128)(2,1)} %bitcast.12, ...), custom_call_target="tpu_custom_call" | custom-call | tf_op jit(solution)/shard_map/pallas_call | solution.py:441
  107.9 1.3 %collective-permute-start = (f32[2,2,128,128]{3,2,1,0:T(8,128)S(1)}, f32[2,2,128,128]{3,2,1,0:T(8,128)S(1)}, u32[]{:S(2)}, u32[]{:S(2)}) collective-permute-start(f32[2,2,128,128]{3,2,1,0:T(8,128)S(1)} %get-tuple-element.21), channel_id=1, source_target_pairs={{2,0},{3,1},{6,4},{7,5}} | collective-permute-start | bytes 786440 | tf_op jit(solution)/shard_map/ppermute | solution.py:449
  109.2 8.5 %shard_map.76 = (bf16[32,12,128,128]{3,2,1,0:T(8,128)(2,1)}, bf16[32,12,128,128]{3,2,1,0:T(8,128)(2,1)}) custom-call(bf16[32,12,128,128]{3,2,1,0:T(8,128)(2,1)S(1)} %get-tuple-element.14.refs_0_, bf16[32,12,128,128]{3,2,1,0:T(8,128)(2,1)S(1)} %get-tuple-element.15.refs_1_), custom_call_target="tpu_custom_call" | custom-call | flops 10000000000 | bytes 25165824 | tf_op jit(solution)/shard_map/pallas_call | solution.py:450
  117.7 0.0 collective-permute-done.received
  117.7 1.3 %shard_map.77 = (bf16[32,128,128]{2,1,0:T(8,128)(2,1)}, bf16[32,128,128]{2,1,0:T(8,128)(2,1)}) custom-call(bf16[32,128,128]{2,1,0:T(8,128)(2,1)S(1)} %get-tuple-element.18.dk_main, bf16[32,128,128]{2,1,0:T(8,128)(2,1)S(1)} %get-tuple-element.19.dv_main, f32[2,2,128,128]{3,2,1,0:T(8,128)S(1)} %get-tuple-element.20.own, ...), custom_call_target="tpu_custom_call" | custom-call | tf_op jit(solution)/shard_map/pallas_call | solution.py:459
Async XLA Ops:
  107.9 9.8 %collective-permute-start = (f32[2,2,128,128]{3,2,1,0:T(8,128)S(1)}, f32[2,2,128,128]{3,2,1,0:T(8,128)S(1)}, u32[]{:S(2)}, u32[]{:S(2)}) collective-permute-start(f32[2,2,128,128]{3,2,1,0:T(8,128)S(1)} %get-tuple-element.21), channel_id=1, source_target_pairs={{2,0},{3,1},{6,4},{7,5}} | collective-permute-start | bytes 786440 | tf_op jit(solution)/shard_map/ppermute | solution.py:449
